TPU v7x, 16 devices: a 4x2x1 block of a 4x4x8 slice. The times are simulated.
16 devices in a mesh: dp: 2 (over y, z), tp: 8 (over x, core).
Axes of the slice: x: 4, y: 2, z: 1, core: 2. Of those that a mesh axis runs over, the one named last changes fastest.
The devices are a block of a 4x4x8 slice.
Arguments:
- hidden: bfloat16 [8192, 768], P(('dp', 'tp')), parts along dimension 0
- targets: int32 [8192], P(('dp', 'tp')), parts along dimension 0
- loss_mask: int32 [8192], P(('dp', 'tp')), parts along dimension 0
- ln_params: float32 [2, 768], replicated
- out_embed: bfloat16 [50304, 768], P('tp')
- ln_mom1: float32 [2, 768], replicated
- ln_mom2: float32 [2, 768], replicated
- embed_mom1: float32 [50304, 768], P('tp')
- embed_mom2: float32 [50304, 768], P('tp')
Outputs:
- output 1: float32 [8192], P(('dp', 'tp')), parts along dimension 0
- output 2: float32 [2], P('dp'), parts along dimension 0
- output 3: bfloat16 [8192, 768], P(('dp', 'tp')), parts along dimension 0
- output 4: float32 [4, 768], P('dp'), parts along dimension 0
- output 5: float32 [4, 768], P('dp'), parts along dimension 0
- output 6: float32 [4, 768], P('dp'), parts along dimension 0
- output 7: bfloat16 [100608, 768], P(('dp', 'tp')), parts along dimension 0
- output 8: float32 [100608, 768], P(('dp', 'tp')), parts along dimension 0
- output 9: float32 [100608, 768], P(('dp', 'tp')), parts along dimension 0
There are 2 independent parts. A program takes and returns all parts, laid end to end along the dimension named above; an argument that names none is the same for every part.
All inputs are finite; a program needn't handle non-finite values.
Results may differ from a plain program's by a relative error of at most 0.001.
Values are sent between devices in bfloat16 or wider.
A program may use at most 768 MiB of HBM per device.

v0:
```python
import jax
import jax.numpy as jnp
from jax import lax
from jax.sharding import PartitionSpec as P

LN_EPS = 1e-5
BETA_ONE = 0.9
BETA_TWO = 0.95
ADAM_EPS = 1e-8
LEARN_RATE = 1e-3
WEIGHT_DECAY = 0.1
ADAM_STEP = 10


def layer_norm(hidden, ln_params):
    rows_f32 = hidden.astype(jnp.float32)
    row_mean = jnp.mean(rows_f32, axis=-1, keepdims=True)
    centered = rows_f32 - row_mean
    row_var = jnp.mean(centered * centered, axis=-1, keepdims=True)
    normed = centered * lax.rsqrt(row_var + LN_EPS)
    return normed * ln_params[0] + ln_params[1]


def adam_step(param_val, grad_val, m_old, v_old, decay_rate):
    m_new = BETA_ONE * m_old + (1.0 - BETA_ONE) * grad_val
    v_new = BETA_TWO * v_old + (1.0 - BETA_TWO) * grad_val * grad_val
    m_hat = m_new / (1.0 - BETA_ONE ** ADAM_STEP)
    v_hat = v_new / (1.0 - BETA_TWO ** ADAM_STEP)
    new_param = param_val - LEARN_RATE * (m_hat / (jnp.sqrt(v_hat) + ADAM_EPS) + decay_rate * param_val)
    return new_param, m_new, v_new


def solution(mesh):
    row_spec = P(("dp", "tp"), None)
    tok_spec = P(("dp", "tp"))
    vocab_spec = P("tp", None)
    repl_spec = P()
    part_spec = P("dp", None)

    def device_step(hidden, targets, loss_mask, ln_params, out_embed, ln_mom1, ln_mom2, embed_mom1, embed_mom2):
        tok_local = hidden.shape[0]
        vocab_local = out_embed.shape[0]
        shard_idx = lax.axis_index("tp")
        x_norm, ln_vjp = jax.vjp(layer_norm, hidden, ln_params)
        x_full = lax.all_gather(x_norm.astype(jnp.bfloat16), "tp", tiled=True)
        tgt_full = lax.all_gather(targets, "tp", tiled=True)
        mask_full = lax.all_gather(loss_mask, "tp", tiled=True).astype(jnp.float32)
        logits = lax.dot_general(x_full, out_embed, (((1,), (1,)), ((), ())), preferred_element_type=jnp.float32)
        local_ids = jnp.arange(vocab_local, dtype=jnp.int32) + shard_idx * vocab_local
        is_target = local_ids[None, :] == tgt_full[:, None]
        local_max = jnp.max(logits, axis=1)
        local_sum = jnp.sum(jnp.exp(logits - local_max[:, None]), axis=1)
        tgt_logit = jnp.sum(jnp.where(is_target, logits, 0.0), axis=1)
        global_max = lax.pmax(local_max, "tp")
        shard_stats = lax.psum(jnp.stack([local_sum * jnp.exp(local_max - global_max), tgt_logit]), "tp")
        log_norm = global_max + jnp.log(shard_stats[0])
        loss_full = (log_norm - shard_stats[1]) * mask_full
        valid_count = jnp.sum(mask_full)
        mean_loss = (jnp.sum(loss_full) / valid_count).reshape(1)
        token_loss = lax.dynamic_slice_in_dim(loss_full, shard_idx * tok_local, tok_local)
        tok_scale = mask_full / valid_count
        d_logits = ((jnp.exp(logits - log_norm[:, None]) - is_target.astype(jnp.float32)) * tok_scale[:, None]).astype(jnp.bfloat16)
        d_embed = lax.dot_general(d_logits, x_full, (((0,), (0,)), ((), ())), preferred_element_type=jnp.float32)
        d_x_part = jnp.dot(d_logits, out_embed, preferred_element_type=jnp.float32)
        d_x = lax.psum_scatter(d_x_part, "tp", scatter_dimension=0, tiled=True)
        d_hidden, d_ln = ln_vjp(d_x)
        d_ln = lax.psum(d_ln, "tp")
        ln_new, ln_mom1_new, ln_mom2_new = adam_step(ln_params, d_ln, ln_mom1, ln_mom2, 0.0)
        embed_f, embed_mom1_new, embed_mom2_new = adam_step(out_embed.astype(jnp.float32), d_embed, embed_mom1, embed_mom2, WEIGHT_DECAY)
        return (token_loss, mean_loss, d_hidden, ln_new, ln_mom1_new, ln_mom2_new, embed_f.astype(jnp.bfloat16), embed_mom1_new, embed_mom2_new)

    return jax.shard_map(device_step, mesh=mesh, in_specs=(row_spec, tok_spec, tok_spec, repl_spec, vocab_spec, repl_spec, repl_spec, vocab_spec, vocab_spec), out_specs=(tok_spec, P("dp"), row_spec, part_spec, part_spec, part_spec, row_spec, row_spec, row_spec), check_vma=False)
```

profile of v0, /device:TPU:113, one launch (start us, length us, event | category | flops | bytes accessed | tf_op | source)
XLA Modules:
  0.0 388.4 jit_solution(1064716143307802312)
XLA Ops:
  7.2 0.1 all-gather.4.cloned.1.call-start
  7.3 0.8 slice_reduce_fusion.1
  8.0 0.0 copy-start.1
  8.1 1.3 convert_reduce_fusion
  9.4 0.0 copy-start.3
  9.4 1.5 fusion.17
  10.9 0.0 copy-start.8
  10.9 0.6 copy-done.8
  11.5 0.0 copy-start.5
  11.5 0.0 copy-done.1
  11.5 0.0 copy-done.3
  11.5 0.6 copy-done.5
  12.1 2.4 fusion.15
  14.4 0.1 all-gather.4.cloned.1.call-update
  14.5 0.1 reduce-scatter.2.cloned.1.call-start
  14.6 20.2 %all-gather.1 = s32[8,1,512]{2,1,0:T(1,128)S(1)} all-gather(s32[1,1,512]{2,1,0:T(1,128)} %bitcast.22), channel_id=1, replica_groups=mesh['dp'=2,'tp'=8] {'tp'}, dimensions={0}, use_global_device_ids=true | all-gather | bytes 18432 | tf_op jit(solution)/shard_map/all_gather | solution.py:47
  34.8 21.8 %all-gather = s32[8,1,512]{2,1,0:T(1,128)S(1)} all-gather(s32[1,1,512]{2,1,0:T(1,128)} %bitcast.23), channel_id=1, replica_groups=mesh['dp'=2,'tp'=8] {'tp'}, dimensions={0}, use_global_device_ids=true | all-gather | bytes 18432 | tf_op jit(solution)/shard_map/all_gather | solution.py:46
  56.6 0.6 convert_reduce_fusion.1
  57.2 0.0 all-gather.4.cloned.1.call-done
  57.2 51.6 %fusion.25 = (f32[4096]{0:T(1024)S(1)}, f32[4096,6288]{0,1:T(8,128)}) fusion(bf16[4096,768]{1,0:T(8,128)(2,1)} %all-gather.4.cloned.1.call-done, bf16[6288,768]{1,0:T(8,128)(2,1)} %param.13), kind=kOutput, calls=%fused_computation.51 | convolution fusion | flops 39586426880 | bytes 118988800 | tf_op jit(solution)/shard_map/dot_general | solution.py:48
  108.9 24.3 %pmax.7 = f32[4096]{0:T(1024)S(1)} all-reduce(f32[4096]{0:T(1024)S(1)} %get-tuple-element.30), channel_id=1, replica_groups=mesh['dp'=2,'tp'=8] {'tp'}, use_global_device_ids=true, to_apply=%region_3.0 | all-reduce | flops 4096 | bytes 32768 | tf_op jit(solution)/shard_map/pmax | solution.py:54
  133.2 33.1 %exponential_reduce_fusion = (f32[4096]{0:T(1024)S(1)}, f32[4096]{0:T(1024)S(1)}) fusion(f32[4096,6288]{0,1:T(8,128)} %get-tuple-element.31, f32[4096]{0:T(1024)S(1)} %get-tuple-element.30, s32[4096]{0:T(1024)S(1)} %bitcast.15, s32[6288]{0:T(1024)S(1)} %iota_add_fusion), kind=kLoop, calls=%fused_computation.6 | loop fusion | flops 128770048 | bytes 103113280 | tf_op jit(solution)/shard_map/reduce_sum | solution.py:52
  166.3 23.9 %psum.14 = f32[2,4096]{1,0:T(2,128)S(1)} all-reduce(f32[2,4096]{1,0:T(2,128)S(1)} %pad_maximum_fusion), channel_id=1, replica_groups=mesh['dp'=2,'tp'=8] {'tp'}, use_global_device_ids=true, to_apply=%region_6.7 | all-reduce | flops 8192 | bytes 65536 | tf_op jit(solution)/shard_map/psum | solution.py:55
  190.2 1.3 fusion.24
  191.5 50.1 %fusion.3 = bf16[4096,6288]{0,1:T(8,128)(2,1)} fusion(f32[4096,6288]{0,1:T(8,128)} %get-tuple-element.31, f32[4096]{0:T(1024)S(1)} %get-tuple-element.29, f32[4096]{0:T(1024)S(1)} %get-tuple-element.26, s32[4096]{0:T(1024)S(1)} %bitcast.16, s32[6288]{0:T(1024)S(1)} %iota_add_fusion), kind=kLoop, calls=%fused_computation.5 | loop fusion | flops 154533888 | bytes 154608192 | tf_op jit(solution)/shard_map/convert_element_type | solution.py:62
  241.6 49.2 %fusion.26 = f32[4096,768]{1,0:T(8,128)} fusion(bf16[4096,6288]{0,1:T(8,128)(2,1)} %fusion.3, bf16[6288,768]{1,0:T(8,128)(2,1)} %param.13), kind=kOutput, calls=%fused_computation.52 | convolution fusion | flops 39560675328 | bytes 73752576 | tf_op jit(solution)/shard_map/dot_general | solution.py:64
  290.9 0.1 reduce-scatter.2.cloned.1.call-update
  292.3 0.7 dynamic_slice.3
  292.9 0.0 copy-start
  292.9 0.0 copy-start.9
  292.9 0.0 copy-start.7
  292.9 0.0 copy-start.10
  293.0 0.0 copy-start.11
  293.0 64.9 %fusion.6 = (bf16[6288,768]{1,0:T(8,128)(2,1)}, f32[6288,768]{1,0:T(8,128)}, f32[6288,768]{1,0:T(8,128)}) fusion(bf16[6288,768]{1,0:T(8,128)(2,1)} %param.13, f32[6288,768]{1,0:T(8,128)} %param.16, f32[6288,768]{1,0:T(8,128)} %param.17, bf16[4096,6288]{0,1:T(8,128)(2,1)} %fusion.3, bf16[4096,768]{1,0:T(8,128)(2,1)} %all-gather.4.cloned.1.call-done), kind=kOutput, calls=%fused_computation.12 | convolution fusion | flops 39642771456 | bytes 154386432 | tf_op jit(solution)/shard_map/dot_general | solution.py:63
  357.9 3.4 reduce-scatter.2.cloned.1.call-done
  361.3 0.0 copy-done
  361.3 0.0 copy-done.2
  361.3 0.0 copy-done.4
  361.3 0.0 copy-done.6
  361.3 2.1 fusion.16
  363.4 0.0 copy-done.9
  363.5 2.1 fusion.23
  365.6 13.1 %psum.15 = f32[2,768]{1,0:T(2,128)S(1)} all-reduce(f32[2,768]{1,0:T(2,128)S(1)} %pad_add_fusion), channel_id=1, replica_groups=mesh['dp'=2,'tp'=8] {'tp'}, use_global_device_ids=true, to_apply=%region_14.15 | all-reduce | flops 1536 | bytes 12288 | tf_op jit(solution)/shard_map/psum | solution.py:67
  378.7 1.0 add_convert_fusion
  379.8 0.0 copy-done.7
  379.8 0.0 copy-done.10
  379.8 0.0 copy-done.11
  379.8 0.6 multiply_subtract_fusion
  (15 shorter events, 0.1 us)
Async XLA Ops:
  7.2 50.1 %all-gather.4.cloned.1.call-start = ((), (), s32[]{:S(2)}) async-start(), calls=%async_computation.1 | async-start | bytes 7077888 | tf_op jit(solution)/shard_map/all_gather | solution.py:45
  8.0 3.4 copy-start.1
  9.4 2.1 copy-start.3
  10.9 0.6 copy-start.8
  11.5 0.6 copy-start.5
  14.5 346.8 %reduce-scatter.2.cloned.1.call-start = ((), (), s32[]{:S(2)}) async-start(), calls=%async_computation.2 | async-start | bytes 14155776 | tf_op jit(solution)/shard_map/reduce_scatter | solution.py:65
  292.9 68.4 %copy-start = (bf16[512,768]{1,0:T(8,128)(2,1)S(1)}, bf16[512,768]{1,0:T(8,128)(2,1)}, u32[]{:S(2)}) copy-start(bf16[512,768]{1,0:T(8,128)(2,1)} %param.9) | copy-start | bytes 2359300
  292.9 68.4 %copy-start.2 = (f32[768]{0:T(1024)S(1)}, f32[768]{0:T(1024)}, u32[]{:S(2)}) copy-start(f32[768]{0:T(1024)} %copy-done.1) | copy-start | bytes 9220
  292.9 68.4 %copy-start.4 = (f32[512]{0:T(512)S(1)}, f32[512]{0:T(512)}, u32[]{:S(2)}) copy-start(f32[512]{0:T(512)} %copy-done.3) | copy-start | bytes 6148
  292.9 68.4 %copy-start.6 = (f32[512]{0:T(512)S(1)}, f32[512]{0:T(512)}, u32[]{:S(2)}) copy-start(f32[512]{0:T(512)} %copy-done.5) | copy-start | bytes 6148
  292.9 70.5 %copy-start.9 = (f32[512]{0:T(512)S(1)}, f32[512]{0:T(512)}, u32[]{:S(2)}) copy-start(f32[512]{0:T(512)} %copy-done.8) | copy-start | bytes 6148
  292.9 86.8 %copy-start.7 = (f32[2,768]{1,0:T(2,128)S(1)}, f32[2,768]{1,0:T(2,128)}, u32[]{:S(2)}) copy-start(f32[2,768]{1,0:T(2,128)} %param.12) | copy-start | bytes 18436
  292.9 86.8 %copy-start.10 = (f32[2,768]{1,0:T(2,128)S(1)}, f32[2,768]{1,0:T(2,128)}, u32[]{:S(2)}) copy-start(f32[2,768]{1,0:T(2,128)} %param.14) | copy-start | bytes 18436
  293.0 86.8 %copy-start.11 = (f32[2,768]{1,0:T(2,128)S(1)}, f32[2,768]{1,0:T(2,128)}, u32[]{:S(2)}) copy-start(f32[2,768]{1,0:T(2,128)} %param.15) | copy-start | bytes 18436
Sparse Core Ops, SparseCore 0:
  14.6 40.0 all-gather.3
  291.0 70.2 reduce-scatter.1
where the time goes:
time: 389 us; the launch traced here: 388 us
  matrix products  166 us (43%)
  blocking collectives  103 us (26%)
  other arithmetic  96.2 us (25%)
  between operations  16.7 us (4%)
    dot_general x1, matrix products, device_step(): lax.dot_general(d_logits, x_full, (((0,), (0,)), ((), ())), preferred_ele...  64.9 us
    dot_general x1, matrix products, device_step(): lax.dot_general(x_full, out_embed, (((1,), (1,)), ((), ())), preferred_el...  51.6 us
    convert_element_type x1, other arithmetic, device_step(): ((jnp.exp(logits - log_norm[:, None]) - is_target.astype(jnp.float32)) *...  50.1 us
    dot_general x1, matrix products, device_step(): d_x_part = jnp.dot(d_logits, out_embed, preferred_element_type=jnp.float32)  49.2 us
    reduce_sum x1, other arithmetic, device_step(): local_sum = jnp.sum(jnp.exp(logits - local_max[:, None]), axis=1)  33.1 us
    pmax x1, blocking collectives, device_step(): global_max = lax.pmax(local_max, 'tp')  24.3 us
    psum x1, blocking collectives, device_step(): lax.psum(jnp.stack([local_sum * jnp.exp(local_max - global_max), tgt_logi...  23.9 us
    all_gather x1, blocking collectives, device_step(): tgt_full = lax.all_gather(targets, 'tp', tiled=True)  21.8 us
  transfers between devices with their start and end apart: 2, of which 1 were waited for; matrix products, arithmetic and copies ran while one was open for 17% of the time, Pallas kernels for 0%

commit v1 on v0

v1 whole, which is shorter than its diff:
```python
import functools

import jax
import jax.numpy as jnp
from jax import lax
from jax.experimental import pallas as pl
from jax.experimental.pallas import tpu as pltpu
from jax.sharding import PartitionSpec as P

LN_EPS = 1e-5
BETA_ONE = 0.9
BETA_TWO = 0.95
ADAM_EPS = 1e-8
LEARN_RATE = 1e-3
WEIGHT_DECAY = 0.1
ADAM_STEP = 10

MESH = pl.DeviceIdType.MESH
VMEM_LIMIT = 64_000_000
NEG = -3.0e38
STAT_ROWS = 64
DOT_ROWS = 1056


def layer_norm(hidden, ln_params):
    rows_f32 = hidden.astype(jnp.float32)
    row_mean = jnp.mean(rows_f32, axis=-1, keepdims=True)
    centered = rows_f32 - row_mean
    row_var = jnp.mean(centered * centered, axis=-1, keepdims=True)
    normed = centered * lax.rsqrt(row_var + LN_EPS)
    return normed * ln_params[0:1] + ln_params[1:2]


def adam_step(param_val, grad_val, m_old, v_old, decay_rate):
    m_new = BETA_ONE * m_old + (1.0 - BETA_ONE) * grad_val
    v_new = BETA_TWO * v_old + (1.0 - BETA_TWO) * grad_val * grad_val
    m_hat = m_new / (1.0 - BETA_ONE ** ADAM_STEP)
    v_hat = v_new / (1.0 - BETA_TWO ** ADAM_STEP)
    new_param = param_val - LEARN_RATE * (m_hat / (jnp.sqrt(v_hat) + ADAM_EPS) + decay_rate * param_val)
    return new_param, m_new, v_new


def row_chunks(rows, size):
    return [(lo, min(size, rows - lo)) for lo in range(0, rows, size)]


def forward_kernel(n, tiles, hid, tm, lnp, e_hbm,
                   z_hbm, x_hbm, lse_o, scale_o, tgt_o, loss_o, mean_o,
                   x_all, x_send, tm_all, e_v, x_t, z_a, z_b, m_run, m_old, s_run, t_run, st_own, st_all,
                   e_sem, z_sem, xo_sem, sx_send, sx_recv, tm_send, tm_recv, st_send, st_recv):
    me = lax.axis_index("tp")
    chips = n // 2
    chip, core = me // 2, lax.rem(me, 2)
    sgn = 1 - 2 * core
    tok = hid.shape[0]
    vocab = e_hbm.shape[0]
    vt = vocab // tiles

    def dev(chip_idx, core_idx):
        return lax.rem(chip_idx + 2 * chips, chips) * 2 + core_idx

    e_copies = [pltpu.make_async_copy(e_hbm.at[pl.ds(t * vt, vt)], e_v.at[pl.ds(t * vt, vt)], e_sem.at[t]) for t in range(tiles)]
    for c in e_copies:
        c.start()

    barrier = pltpu.get_barrier_semaphore()
    for r in range(1, n):
        pl.semaphore_signal(barrier, inc=1, device_id={"tp": lax.rem(me + r, n)}, device_id_type=MESH)

    x_send[...] = layer_norm(hid[...], lnp[...]).astype(jnp.bfloat16)
    x_all[me] = x_send[...]
    tm_all[me] = tm[...]
    pl.semaphore_wait(barrier, n - 1)

    def xcopy(idx, src, slot, dst, recv):
        return pltpu.make_async_remote_copy(src_ref=src, dst_ref=x_all.at[slot], send_sem=sx_send.at[idx],
                                            recv_sem=sx_recv.at[recv], device_id={"tp": dst}, device_id_type=MESH)

    partner = dev(chip, 1 - core)
    ahead = dev(chip + sgn, core)
    behind = dev(chip - sgn, core)
    a1 = dev(chip - sgn, core)
    a2 = dev(chip + sgn, core)
    far = dev(chip + 2, core)
    s0 = xcopy(0, x_send, me, partner, 1)
    s1 = xcopy(1, x_send, me, ahead, 2)
    s2 = xcopy(2, x_send, me, behind, 4)
    s3 = xcopy(3, x_all.at[a1], a1, partner, 3)
    s4 = xcopy(4, x_all.at[a1], a1, ahead, 6)
    s5 = xcopy(5, x_all.at[a2], a2, partner, 5)
    s6 = xcopy(6, x_all.at[far], far, partner, 7)

    def tmcopy(r):
        peer = lax.rem(me + r, n)
        return pltpu.make_async_remote_copy(src_ref=tm, dst_ref=tm_all.at[me], send_sem=tm_send.at[r - 1],
                                            recv_sem=tm_recv.at[r - 1], device_id={"tp": peer}, device_id_type=MESH)

    tm_copies = [tmcopy(r) for r in range(1, n)]
    s0.start()
    for c in tm_copies:
        c.start()
    s1.start()
    for c in tm_copies:
        c.wait()

    def block_of(p):
        q = lax.rem(p, 2)
        h = p // 2
        own_core = core + q * sgn
        step = jnp.where(h == 0, 0, jnp.where(h == 1, -sgn, jnp.where(h == 2, sgn, 2)))
        flip = jnp.where(h == 3, 1, 1 - 2 * q)
        return dev(chip + step * flip, own_core)

    def z_copy(nn, buf):
        p, t = nn // tiles, lax.rem(nn, tiles)
        slot = lax.rem(nn, 2)
        return pltpu.make_async_copy(buf, z_hbm.at[block_of(p), pl.ds(pl.multiple_of(t * vt, 16), vt)], z_sem.at[slot])

    def x_out(p):
        b = block_of(p)
        return pltpu.make_async_copy(x_all.at[b], x_hbm.at[b], xo_sem.at[p])

    def reset():
        m_run[...] = jnp.full_like(m_run, NEG)
        m_old[...] = jnp.full_like(m_old, NEG)
        s_run[...] = jnp.zeros_like(s_run)
        t_run[...] = jnp.zeros_like(t_run)

    sub = lax.broadcasted_iota(jnp.int32, (8, tok), 0)

    def sums_begin(nn):
        p, t = nn // tiles, lax.rem(nn, tiles)
        want = tm_all[block_of(p)][0:1] - (me * vocab + t * vt) - sub
        m = m_run[...]
        return want, m, s_run[...] * jnp.exp(m_old[...] - m), t_run[...]

    def sums_rows(acc, buf, start, count):
        want, m, s, tgt = acc
        for lo, size in row_chunks(count, STAT_ROWS):
            z = buf[start + lo:start + lo + size, :].reshape(size // 8, 8, tok)
            s = s + jnp.sum(jnp.exp(z - m[None]), axis=0)
            rows = lax.broadcasted_iota(jnp.int32, z.shape, 0) * 8 + (start + lo)
            tgt = tgt + jnp.sum(jnp.where(want[None] == rows, z, 0.0), axis=0)
        return want, m, s, tgt

    def sums_end(acc):
        _, m_old[...], s_run[...], t_run[...] = acc

    def sums(nn, buf):
        sums_end(sums_rows(sums_begin(nn), buf, 0, vt))

    def st_copy(r, blk):
        peer = lax.rem(me + r, n)
        return pltpu.make_async_remote_copy(src_ref=st_own.at[blk], dst_ref=st_all.at[me, blk], send_sem=st_send.at[r - 1],
                                            recv_sem=st_recv.at[r - 1], device_id={"tp": peer}, device_id_type=MESH)

    def finish(p):
        b = block_of(p)
        m, s = m_run[...], s_run[...]
        m_all = jnp.max(m, axis=0, keepdims=True)
        s_sum = jnp.sum(s * jnp.exp(m - m_all), axis=0, keepdims=True)
        both = jnp.concatenate([m_all + jnp.log(s_sum), jnp.sum(t_run[...], axis=0, keepdims=True)], axis=0)
        st_own[b] = both
        st_all[me, b] = both

    def send_stats(p):
        b = block_of(p)
        for r in range(1, n):
            st_copy(r, b).start()

    reset()

    def step(nn, cur, prev):
        p, t = nn // tiles, lax.rem(nn, tiles)

        @pl.when(t == 0)
        def _():
            @pl.when(p == 1)
            def _():
                s0.wait_recv()

            @pl.when(p == 2)
            def _():
                s1.wait()
                s3.start()
                s2.start()

            @pl.when(p == 3)
            def _():
                s3.wait_recv()
                s4.start()

            @pl.when(p == 4)
            def _():
                s2.wait()
                s5.start()

            @pl.when(p == 5)
            def _():
                s5.wait_recv()

            @pl.when(p == 6)
            def _():
                s4.wait_recv()
                s6.start()

            @pl.when(p == 7)
            def _():
                s6.wait_recv()

            b = block_of(p)
            x_out(p).start()
            x_t[...] = x_all[b].T

        for tt in range(tiles):
            @pl.when(nn == tt)
            def _():
                e_copies[tt].wait()

        @pl.when(nn >= 2)
        def _():
            z_copy(nn - 2, cur).wait()

        top = jnp.full((8, tok), NEG, jnp.float32)
        acc = sums_begin(jnp.maximum(nn - 1, 0))
        for lo, size in row_chunks(vt, DOT_ROWS):
            z = jnp.dot(e_v[pl.ds(pl.multiple_of(t * vt + lo, 16), size), :], x_t[...], preferred_element_type=jnp.float32)
            cur[lo:lo + size, :] = z
            top = jnp.maximum(top, jnp.max(z.reshape(size // 8, 8, tok), axis=0))
            acc = sums_rows(acc, prev, lo, size)
        sums_end(acc)
        z_copy(nn, cur).start()

        @pl.when(t == 0)
        def _():
            @pl.when(nn > 0)
            def _():
                finish(p - 1)
            reset()

        m_run[...] = jnp.maximum(m_run[...], top)

        @pl.when((t == 1) & (p > 0))
        def _():
            send_stats(p - 1)

    def body(i, carry):
        step(2 * i, z_a, z_b)
        step(2 * i + 1, z_b, z_a)
        return carry

    total = n * tiles
    lax.fori_loop(0, total // 2, body, 0)
    sums(total - 1, z_b)
    finish(n - 1)
    z_copy(total - 2, z_a).wait()
    send_stats(n - 1)
    z_copy(total - 1, z_b).wait()
    for c in (s0, s2, s3, s4, s5, s6):
        pass
    s0.wait_send()
    s3.wait_send()
    s4.wait_send()
    s5.wait_send()
    s6.wait_send()
    for p in range(n):
        x_out(p).wait()

    for r in range(1, n):
        src = lax.rem(me + n - r, n)
        pltpu.make_async_remote_copy(src_ref=st_own, dst_ref=st_all.at[src], send_sem=st_send.at[r - 1],
                                     recv_sem=st_recv.at[r - 1], device_id={"tp": src}, device_id_type=MESH).wait()

    parts = [st_all[d] for d in range(n)]
    lses = [q[:, 0, :] for q in parts]
    top = functools.reduce(jnp.maximum, lses)
    lse = top + jnp.log(sum(jnp.exp(q - top) for q in lses))
    tgt_logit = sum(q[:, 1, :] for q in parts)
    tm_full = tm_all[...]
    mask = tm_full[:, 1, :].astype(jnp.float32)
    count = jnp.sum(mask)
    loss = (lse - tgt_logit) * mask
    lse_o[...] = lse
    scale_o[...] = mask / count
    tgt_o[...] = tm_full[:, 0, :] - me * vocab
    own = lax.broadcasted_iota(jnp.int32, loss.shape, 0) == me
    loss_o[...] = jnp.sum(jnp.where(own, loss, 0.0), axis=0, keepdims=True)
    mean_o[...] = jnp.full(mean_o.shape, jnp.sum(loss) / count, jnp.float32)


def forward(n, hidden, tm, ln_params, out_embed):
    tok, dim = hidden.shape
    vocab = out_embed.shape[0]
    tiles = 3
    vt = vocab // tiles
    vmem = pl.BlockSpec(memory_space=pltpu.VMEM)
    hbm = pl.BlockSpec(memory_space=pl.ANY)
    f32, bf16, i32 = jnp.float32, jnp.bfloat16, jnp.int32
    dma = pltpu.SemaphoreType.DMA
    return pl.pallas_call(
        functools.partial(forward_kernel, n, tiles),
        name="forward",
        out_shape=(
            jax.ShapeDtypeStruct((n, vocab, tok), f32),
            jax.ShapeDtypeStruct((n, tok, dim), bf16),
            jax.ShapeDtypeStruct((n, tok), f32),
            jax.ShapeDtypeStruct((n, tok), f32),
            jax.ShapeDtypeStruct((n, tok), i32),
            jax.ShapeDtypeStruct((1, tok), f32),
            jax.ShapeDtypeStruct((1, 128), f32),
        ),
        in_specs=[vmem, vmem, vmem, hbm],
        out_specs=(hbm, hbm, vmem, vmem, vmem, vmem, vmem),
        scratch_shapes=[
            pltpu.VMEM((n, tok, dim), bf16),
            pltpu.VMEM((tok, dim), bf16),
            pltpu.VMEM((n, 2, tok), i32),
            pltpu.VMEM((vocab, dim), bf16),
            pltpu.VMEM((dim, tok), bf16),
            pltpu.VMEM((vt, tok), f32),
            pltpu.VMEM((vt, tok), f32),
            pltpu.VMEM((8, tok), f32),
            pltpu.VMEM((8, tok), f32),
            pltpu.VMEM((8, tok), f32),
            pltpu.VMEM((8, tok), f32),
            pltpu.VMEM((n, 2, tok), f32),
            pltpu.VMEM((n, n, 2, tok), f32),
            dma((tiles,)), dma((2,)), dma((n,)),
            dma((7,)), dma((8,)), dma((n - 1,)), dma((n - 1,)), dma((n - 1,)), dma((n - 1,)),
        ],
        compiler_params=pltpu.CompilerParams(collective_id=0, has_side_effects=True, vmem_limit_bytes=VMEM_LIMIT),
        cost_estimate=pl.CostEstimate(flops=2 * n * tok * dim * vocab, bytes_accessed=4 * n * tok * vocab, transcendentals=n * tok * vocab),
    )(hidden, tm, ln_params, out_embed)


def dx_kernel(z, e, lse, scale, tgt, dz_o, dx_o, e_t):
    b, t = pl.program_id(0), pl.program_id(1)
    vt, tok = z.shape

    @pl.when(b == 0)
    def _():
        e_t[t] = e[...].T

    l, sc = lse[...], scale[...]
    want = tgt[...] - t * vt
    for lo, size in row_chunks(vt, 128):
        rows = lax.broadcasted_iota(jnp.int32, (size, tok), 0) + lo
        hot = jnp.where(rows == want, 1.0, 0.0)
        dz_o[lo:lo + size, :] = ((jnp.exp(z[lo:lo + size, :] - l) - hot) * sc).astype(jnp.bfloat16)
    part = jnp.dot(e_t[t], dz_o[...], preferred_element_type=jnp.float32)

    @pl.when(t == 0)
    def _():
        dx_o[...] = part

    @pl.when(t > 0)
    def _():
        dx_o[...] += part


def dz_dx(z, out_embed, lse, scale, tgt):
    n, vocab, tok = z.shape
    dim = out_embed.shape[1]
    tiles = 3
    vt = vocab // tiles
    f32, bf16 = jnp.float32, jnp.bfloat16
    row = pl.BlockSpec((None, 1, tok), lambda b, t: (b, 0, 0))
    return pl.pallas_call(
        dx_kernel,
        name="dz_dx",
        grid=(n, tiles),
        in_specs=[
            pl.BlockSpec((None, vt, tok), lambda b, t: (b, t, 0)),
            pl.BlockSpec((vt, dim), lambda b, t: (jnp.where(b == 0, t, tiles - 1), 0)),
            row, row, row,
        ],
        out_specs=(
            pl.BlockSpec((vt, tok), lambda b, t: (t, b)),
            pl.BlockSpec((None, dim, tok), lambda b, t: (b, 0, 0)),
        ),
        out_shape=(jax.ShapeDtypeStruct((vocab, n * tok), bf16), jax.ShapeDtypeStruct((n, dim, tok), f32)),
        scratch_shapes=[pltpu.VMEM((tiles, dim, vt), bf16)],
        compiler_params=pltpu.CompilerParams(vmem_limit_bytes=VMEM_LIMIT, dimension_semantics=("arbitrary", "arbitrary")),
        cost_estimate=pl.CostEstimate(flops=2 * n * tok * dim * vocab, bytes_accessed=6 * n * tok * vocab, transcendentals=n * tok * vocab),
    )(z, out_embed, lse.reshape(n, 1, tok), scale.reshape(n, 1, tok), tgt.reshape(n, 1, tok))


def update_kernel(dz, x, e, m, v, e_o, m_o, v_o, grad):
    i = pl.program_id(0)
    last = pl.num_programs(0) - 1

    def adam():
        g = grad[lax.rem(i + 1, 2)]
        new_e, m_o[...], v_o[...] = adam_step(e[...].astype(jnp.float32), g, m[...], v[...], WEIGHT_DECAY)
        e_o[...] = new_e.astype(jnp.bfloat16)

    @pl.when(i < last)
    def _():
        grad[lax.rem(i, 2)] = jnp.dot(dz[...], x[...], preferred_element_type=jnp.float32)
        adam()

    @pl.when(i == last)
    def _():
        adam()


def update(dz, x, out_embed, mom1, mom2):
    vocab, dim = out_embed.shape
    toks = x.shape[0]
    vt = 640
    steps = pl.cdiv(vocab, vt)
    f32, bf16 = jnp.float32, jnp.bfloat16
    late = pl.BlockSpec((vt, dim), lambda i: (jnp.maximum(i - 1, 0), 0))
    return pl.pallas_call(
        update_kernel,
        name="update",
        grid=(steps + 1,),
        in_specs=[
            pl.BlockSpec((vt, toks), lambda i: (jnp.minimum(i, steps - 1), 0)),
            pl.BlockSpec((toks, dim), lambda i: (0, 0)),
            late, late, late,
        ],
        out_specs=(late, late, late),
        out_shape=(jax.ShapeDtypeStruct((vocab, dim), bf16), jax.ShapeDtypeStruct((vocab, dim), f32), jax.ShapeDtypeStruct((vocab, dim), f32)),
        scratch_shapes=[pltpu.VMEM((2, vt, dim), f32)],
        compiler_params=pltpu.CompilerParams(vmem_limit_bytes=VMEM_LIMIT, dimension_semantics=("arbitrary",)),
        cost_estimate=pl.CostEstimate(flops=2 * toks * dim * vocab, bytes_accessed=2 * toks * vocab + 20 * vocab * dim, transcendentals=2 * vocab * dim),
    )(dz, x, out_embed, mom1, mom2)


def solution(mesh):
    n = mesh.shape["tp"]
    row_spec = P(("dp", "tp"), None)
    tok_spec = P(("dp", "tp"))
    vocab_spec = P("tp", None)
    repl_spec = P()
    part_spec = P("dp", None)

    def device_step(hidden, targets, loss_mask, ln_params, out_embed, ln_mom1, ln_mom2, embed_mom1, embed_mom2):
        tok, dim = hidden.shape
        tm = jnp.stack([targets, loss_mask])
        z, x_full, lse, scale, tgt, loss, mean = forward(n, hidden, tm, ln_params, out_embed)
        dz, dx = dz_dx(z, out_embed, lse, scale, tgt)
        d_x_t = lax.psum_scatter(dx, "tp", scatter_dimension=0, tiled=False)
        embed_new, embed_mom1_new, embed_mom2_new = update(dz, x_full.reshape(n * tok, dim), out_embed, embed_mom1, embed_mom2)
        _, ln_vjp = jax.vjp(layer_norm, hidden, ln_params)
        d_hidden, d_ln = ln_vjp(d_x_t.T)
        d_ln = lax.psum(d_ln, "tp")
        ln_new, ln_mom1_new, ln_mom2_new = adam_step(ln_params, d_ln, ln_mom1, ln_mom2, 0.0)
        return (loss.reshape(tok), mean[0, :1], d_hidden, ln_new, ln_mom1_new, ln_mom2_new, embed_new, embed_mom1_new, embed_mom2_new)

    return jax.shard_map(device_step, mesh=mesh, in_specs=(row_spec, tok_spec, tok_spec, repl_spec, vocab_spec, repl_spec, repl_spec, vocab_spec, vocab_spec), out_specs=(tok_spec, P("dp"), row_spec, part_spec, part_spec, part_spec, row_spec, row_spec, row_spec), check_vma=False)
```

time: 389 us -> 257 us (0.66)
  Pallas kernels: 0 us -> 215 us
  matrix products: 166 us -> 0 us
  other arithmetic: 96.2 us -> 5.36 us
  blocking collectives: 103 us -> 12.4 us
  local copies, waits for them, and re-layouts: 2.69 us -> 7.54 us
    pallas_call x0 -> x3, Pallas kernels: none -> 215 us  [the longest x1 74.4 us: dz_dx(): pl.pallas_call(dx_kernel, name='dz_dx', grid=(n, tiles), in_specs=[pl.Blo...]
    dot_general x3 -> x0, matrix products: 166 us -> none  [the longest x1 64.9 us: device_step(): lax.dot_general(d_logits, x_full, (((0,), (0,)), ((), ())), preferred_ele...]
    convert_element_type x3 -> x0, other arithmetic: 52.5 us -> none  [the longest x1 50.1 us: device_step(): ((jnp.exp(logits - log_norm[:, None]) - is_target.astype(jnp.float32)) *...]
    all_gather x2 -> x0, blocking collectives: 42 us -> none  [the longest x1 21.8 us: device_step(): tgt_full = lax.all_gather(targets, 'tp', tiled=True)]
    reduce_sum x5 -> x2, other arithmetic: 39.2 us -> 0.86 us  [layer_norm(): return normed * ln_params[0:1] + ln_params[1:2]]
    pmax x1 -> x0, blocking collectives: 24.3 us -> none  [device_step(): global_max = lax.pmax(local_max, 'tp')]
    psum x1 -> x0, blocking collectives: 23.9 us -> none  [device_step(): lax.psum(jnp.stack([local_sum * jnp.exp(local_max - global_max), tgt_logi...]
    reshape x2 -> x5, local copies, waits for them, and re-layouts: 0.01 us -> 4.01 us  [the longest x1 1.33 us: dz_dx(): lse.reshape(n, 1, tok)]
  transfers between devices with their start and end apart: 2 -> 1, of which waited for: 1 -> 0; matrix products, arithmetic and copies ran while one was open for 17% -> 0% of each run, Pallas kernels for 0% -> 27%
where the time goes in v1:
time: 257 us; the launch traced here: 255 us
  Pallas kernels  215 us (84%)
  between operations  15.3 us (6%)
  blocking collectives  12.4 us (5%)
  local copies, waits for them, and re-layouts  7.54 us (3%)
  other arithmetic  5.36 us (2%)
    pallas_call x1, Pallas kernels, dz_dx(): pl.pallas_call(dx_kernel, name='dz_dx', grid=(n, tiles), in_specs=[pl.Blo...  74.4 us
    pallas_call x1, Pallas kernels, forward(): pl.pallas_call(functools.partial(forward_kernel, n, tiles), name='forward...  72.4 us
    pallas_call x1, Pallas kernels, update(): pl.pallas_call(update_kernel, name='update', grid=(steps + 1,), in_specs=...  67.7 us
    psum x1, blocking collectives, device_step(): d_ln = lax.psum(d_ln, 'tp')  12.4 us
  transfers between devices with their start and end apart: 1, of which 0 were waited for; matrix products, arithmetic and copies ran while one was open for 0% of the time, Pallas kernels for 27%

profile of v1, /device:TPU:113, one launch (start us, length us, event | category | flops | bytes accessed | tf_op | source)
XLA Modules:
  0.0 255.4 jit_solution(14744660672876051859)
XLA Ops:
  7.2 0.1 reduce-scatter.2.cloned.1.call-start
  7.3 1.3 pad_add_fusion.1.tm
  8.6 72.4 %forward.1 = (f32[8,6288,512]{2,1,0:T(8,128)}, bf16[8,512,768]{2,1,0:T(8,128)(2,1)}, f32[8,512]{1,0:T(8,128)}, f32[8,512]{1,0:T(8,128)}, s32[8,512]{1,0:T(8,128)}, /*index=5*/f32[1,512]{1,0:T(1,128)}, f32[1,128]{1,0:T(1,128)}) custom-call(bf16[512,768]{1,0:T(8,128)(2,1)} %hid.1, s32[2,512]{1,0:T(2,128)} %pad_add_fusion.1.tm, f32[2,768]{1,0:T(2,128)} %lnp.1, ...), custom_call_target="tpu_custom_call" | custom-call | flops 39560675328 | bytes 103022592 | tf_op jit(solution)/shard_map/forward/pallas_call | solution.py:300
  81.0 1.3 reshape.64.lse
  82.3 1.3 reshape.65.scale
  83.6 1.3 reshape.66.tgt
  85.0 74.4 %dz_dx.1 = (bf16[6288,4096]{1,0:T(8,128)(2,1)}, f32[8,768,512]{2,1,0:T(8,128)}) custom-call(f32[8,6288,512]{2,1,0:T(8,128)} %get-tuple-element.23.z, bf16[6288,768]{1,0:T(8,128)(2,1)} %e.3, f32[8,1,512]{2,1,0:T(1,128)} %reshape.64.lse, f32[8,1,512]{2,1,0:T(1,128)} %reshape.65.scale, s32[8,1,512]{2,1,0:T(1,128)} %reshape.66.tgt), custom_call_target="tpu_custom_call" | custom-call | flops 39560675328 | bytes 154533888 | tf_op jit(solution)/shard_map/dz_dx/pallas_call | solution.py:368
  159.4 0.0 copy-start.1
  159.4 0.1 reduce-scatter.2.cloned.1.call-update
  159.5 1.1 copy-done.1
  160.5 0.0 copy-start.2
  160.6 0.3 copy.18
  160.8 0.4 copy-done.2
  161.3 0.2 convert_reduce_fusion
  161.4 67.7 %update.1 = (bf16[6288,768]{1,0:T(8,128)(2,1)}, f32[6288,768]{1,0:T(8,128)}, f32[6288,768]{1,0:T(8,128)}) custom-call(bf16[6288,4096]{1,0:T(8,128)(2,1)} %get-tuple-element.28.dz, bf16[4096,768]{1,0:T(8,128)(2,1)} %bitcast.22, bf16[6288,768]{1,0:T(8,128)(2,1)} %e.3, f32[6288,768]{1,0:T(8,128)} %m.1, f32[6288,768]{1,0:T(8,128)} %v.1), custom_call_target="tpu_custom_call" | custom-call | flops 39560675328 | bytes 148094976 | tf_op jit(solution)/shard_map/update/pallas_call | solution.py:414
  229.2 0.0 reduce-scatter.2.cloned.1.call-done
  229.2 0.0 copy-start
  229.2 1.9 fusion.4
  231.1 0.0 copy-done
  231.1 0.7 fusion.7
  231.8 0.2 reduce_sum.66
  232.0 12.4 %psum.7 = f32[2,768]{1,0:T(2,128)S(1)} all-reduce(f32[2,768]{1,0:T(2,128)S(1)} %pad_add_fusion), channel_id=1, replica_groups=mesh['dp'=2,'tp'=8] {'tp'}, use_global_device_ids=true, to_apply=%region_7.0 | all-reduce | flops 1536 | bytes 12288 | tf_op jit(solution)/shard_map/psum | solution.py:448
  244.5 0.5 add_convert_fusion
  244.9 0.0 copy-start.3
  244.9 0.0 copy-start.4
  245.0 0.0 copy-start.5
  245.0 0.0 copy-start.6
  245.0 1.2 copy.19
  246.1 0.0 copy-done.3
  246.1 0.0 copy-done.4
  246.1 0.6 multiply_subtract_fusion
  246.8 0.0 copy-done.5
  246.8 0.6 copy.22
  247.3 0.0 copy-done.6
  (7 shorter events, 0.1 us)
Async XLA Ops:
  7.2 222.0 %reduce-scatter.2.cloned.1.call-start = ((), (), s32[]{:S(2)}) async-start(), calls=%async_computation.1 | async-start | bytes 14155776 | tf_op jit(solution)/shard_map/reduce_scatter | solution.py:444
  159.4 1.1 copy-start.1
  160.5 0.7 copy-start.2
  229.2 1.9 copy-start
  244.9 1.2 copy-start.3
  244.9 1.2 copy-start.4
  245.0 1.8 copy-start.5
  245.0 2.4 copy-start.6
Sparse Core Ops, SparseCore 0:
  159.6 67.7 reduce-scatter.1

commit v2 on v1

--- a/solution.py
+++ b/solution.py
@@ -19,6 +19,7 @@
 VMEM_LIMIT = 64_000_000
 NEG = -3.0e38
 STAT_ROWS = 64
+ADAM_ROWS = 64
 DOT_ROWS = 1056
 
 
@@ -256,8 +257,6 @@
     z_copy(total - 2, z_a).wait()
     send_stats(n - 1)
     z_copy(total - 1, z_b).wait()
-    for c in (s0, s2, s3, s4, s5, s6):
-        pass
     s0.wait_send()
     s3.wait_send()
     s4.wait_send()
@@ -280,9 +279,10 @@
     mask = tm_full[:, 1, :].astype(jnp.float32)
     count = jnp.sum(mask)
     loss = (lse - tgt_logit) * mask
-    lse_o[...] = lse
-    scale_o[...] = mask / count
-    tgt_o[...] = tm_full[:, 0, :] - me * vocab
+    for d in range(n):
+        lse_o[d] = lse[d:d + 1]
+        scale_o[d] = mask[d:d + 1] / count
+        tgt_o[d] = tm_full[d, 0:1, :] - me * vocab
     own = lax.broadcasted_iota(jnp.int32, loss.shape, 0) == me
     loss_o[...] = jnp.sum(jnp.where(own, loss, 0.0), axis=0, keepdims=True)
     mean_o[...] = jnp.full(mean_o.shape, jnp.sum(loss) / count, jnp.float32)
@@ -303,9 +303,9 @@
         out_shape=(
             jax.ShapeDtypeStruct((n, vocab, tok), f32),
             jax.ShapeDtypeStruct((n, tok, dim), bf16),
-            jax.ShapeDtypeStruct((n, tok), f32),
-            jax.ShapeDtypeStruct((n, tok), f32),
-            jax.ShapeDtypeStruct((n, tok), i32),
+            jax.ShapeDtypeStruct((n, 1, tok), f32),
+            jax.ShapeDtypeStruct((n, 1, tok), f32),
+            jax.ShapeDtypeStruct((n, 1, tok), i32),
             jax.ShapeDtypeStruct((1, tok), f32),
             jax.ShapeDtypeStruct((1, 128), f32),
         ),
@@ -333,75 +333,214 @@
     )(hidden, tm, ln_params, out_embed)
 
 
-def dx_kernel(z, e, lse, scale, tgt, dz_o, dx_o, e_t):
-    b, t = pl.program_id(0), pl.program_id(1)
-    vt, tok = z.shape
-
-    @pl.when(b == 0)
-    def _():
-        e_t[t] = e[...].T
-
-    l, sc = lse[...], scale[...]
-    want = tgt[...] - t * vt
-    for lo, size in row_chunks(vt, 128):
-        rows = lax.broadcasted_iota(jnp.int32, (size, tok), 0) + lo
-        hot = jnp.where(rows == want, 1.0, 0.0)
-        dz_o[lo:lo + size, :] = ((jnp.exp(z[lo:lo + size, :] - l) - hot) * sc).astype(jnp.bfloat16)
-    part = jnp.dot(e_t[t], dz_o[...], preferred_element_type=jnp.float32)
-
-    @pl.when(t == 0)
-    def _():
-        dx_o[...] = part
-
-    @pl.when(t > 0)
-    def _():
-        dx_o[...] += part
-
-
-def dz_dx(z, out_embed, lse, scale, tgt):
-    n, vocab, tok = z.shape
-    dim = out_embed.shape[1]
+def backward_kernel(n, tiles, hid, lnp, lnm1, lnm2, lse, scale, tgt, z_hbm, e_hbm,
+                    dz_hbm, dh_o, lnp_o, lnm1_o, lnm2_o,
+                    z_0, z_1, z_2, dz_0, dz_1, dz_2, e_in, e_t, acc, to_pair, from_pair, to_ring, from_ring, d_ln,
+                    z_sem, dz_sem, e_sem, pair_send, pair_recv, ring_send, ring_recv, ln_send, ln_recv):
+    me = lax.axis_index("tp")
+    chips = n // 2
+    chip, core = me // 2, lax.rem(me, 2)
+    sgn = 1 - 2 * core
+    vt, tok = z_0.shape
+    z_bufs, dz_bufs = (z_0, z_1, z_2), (dz_0, dz_1, dz_2)
+
+    def dev(chip_idx, core_idx):
+        return lax.rem(chip_idx + 2 * chips, chips) * 2 + core_idx
+
+    partner = dev(chip, 1 - core)
+    ahead = dev(chip + sgn, core)
+
+    def block_of(q):
+        s, own = q // 2, lax.rem(q, 2)
+        return dev(chip + sgn * (1 + s) * (1 - 2 * own), jnp.where(own == 1, core, 1 - core))
+
+    def z_copy(q, t):
+        return pltpu.make_async_copy(z_hbm.at[block_of(q), pl.ds(t * vt, vt)], z_bufs[t], z_sem.at[t])
+
+    def dz_copy(q, t):
+        cols = pl.ds(pl.multiple_of(block_of(q) * tok, tok), tok)
+        return pltpu.make_async_copy(dz_bufs[t], dz_hbm.at[pl.ds(t * vt, vt), cols], dz_sem.at[t])
+
+    e_copies = [pltpu.make_async_copy(e_hbm.at[pl.ds(t * vt, vt)], e_in.at[pl.ds(t * vt, vt)], e_sem.at[t]) for t in range(tiles)]
+    for t in range(tiles):
+        e_copies[t].start()
+        z_copy(0, t).start()
+
+    barrier = pltpu.get_barrier_semaphore()
+    for r in range(1, n):
+        pl.semaphore_signal(barrier, inc=1, device_id={"tp": lax.rem(me + r, n)}, device_id_type=MESH)
+    pl.semaphore_wait(barrier, n - 1)
+
+    def pair_copy(s):
+        return pltpu.make_async_remote_copy(src_ref=to_pair.at[lax.rem(s, 2)], dst_ref=from_pair.at[s], send_sem=pair_send.at[s],
+                                            recv_sem=pair_recv.at[s], device_id={"tp": partner}, device_id_type=MESH)
+
+    def ring_copy(s):
+        return pltpu.make_async_remote_copy(src_ref=to_ring.at[lax.rem(s, 2)], dst_ref=from_ring.at[s], send_sem=ring_send.at[s],
+                                            recv_sem=ring_recv.at[s], device_id={"tp": ahead}, device_id_type=MESH)
+
+    last_step = chips - 1
+
+    def tile_step(q, t, l, sc, want):
+        z, dz = z_bufs[t], dz_bufs[t]
+
+        @pl.when(q == 0)
+        def _():
+            e_copies[t].wait()
+            e_t[t] = e_in[t * vt:(t + 1) * vt, :].T
+
+        @pl.when(q > 0)
+        def _():
+            dz_copy(q - 1, t).wait()
+
+        z_copy(q, t).wait()
+        for lo, size in row_chunks(vt, 128):
+            rows = lax.broadcasted_iota(jnp.int32, (size, tok), 0) + (t * vt + lo)
+            hot = jnp.where(rows == want, 1.0, 0.0)
+            dz[lo:lo + size, :] = ((jnp.exp(z[lo:lo + size, :] - l) - hot) * sc).astype(jnp.bfloat16)
+        part = jnp.dot(e_t[t], dz[...], preferred_element_type=jnp.float32)
+        if t == 0:
+            acc[...] = part
+        else:
+            acc[...] += part
+        dz_copy(q, t).start()
+
+        @pl.when(q < n - 1)
+        def _():
+            z_copy(q + 1, t).start()
+
+    def body(q, carry):
+        b = block_of(q)
+        l, sc, want = lse[b], scale[b], tgt[b]
+        for t in range(tiles):
+            tile_step(q, t, l, sc, want)
+        s = q // 2
+
+        @pl.when(lax.rem(q, 2) == 0)
+        def _():
+            @pl.when(s >= 2)
+            def _():
+                pair_copy(s - 2).wait_send()
+            to_pair[lax.rem(s, 2)] = acc[...]
+            pair_copy(s).start()
+
+        @pl.when(lax.rem(q, 2) == 1)
+        def _():
+            pair_copy(s).wait_recv()
+            acc[...] += from_pair[s]
+
+            @pl.when(s > 0)
+            def _():
+                ring_copy(s - 1).wait_recv()
+                acc[...] += from_ring[s - 1]
+
+            @pl.when(s < last_step)
+            def _():
+                @pl.when(s >= 2)
+                def _():
+                    ring_copy(s - 2).wait_send()
+                to_ring[lax.rem(s, 2)] = acc[...]
+                ring_copy(s).start()
+
+        return carry
+
+    lax.fori_loop(0, n, body, 0)
+    for s in (last_step - 1, last_step):
+        pair_copy(s).wait_send()
+    for s in range(max(last_step - 2, 0), last_step):
+        ring_copy(s).wait_send()
+    for t in range(tiles):
+        dz_copy(n - 1, t).wait()
+
+    d_x = acc[...].T
+    rows = hid[...].astype(jnp.float32)
+    centered = rows - jnp.mean(rows, axis=-1, keepdims=True)
+    rstd = lax.rsqrt(jnp.mean(centered * centered, axis=-1, keepdims=True) + LN_EPS)
+    normed = centered * rstd
+    gain = lnp[0:1, :]
+    d_ln[me] = jnp.concatenate([jnp.sum(d_x * normed, axis=0, keepdims=True), jnp.sum(d_x, axis=0, keepdims=True)], axis=0)
+
+    def ln_copy(r, slot, peer):
+        return pltpu.make_async_remote_copy(src_ref=d_ln.at[slot], dst_ref=d_ln.at[slot], send_sem=ln_send.at[r - 1],
+                                            recv_sem=ln_recv.at[r - 1], device_id={"tp": peer}, device_id_type=MESH)
+
+    d_normed = d_x * gain
+    proj = jnp.mean(d_normed * normed, axis=-1, keepdims=True)
+    dh_o[...] = (rstd * (d_normed - jnp.mean(d_normed, axis=-1, keepdims=True) - normed * proj)).astype(jnp.bfloat16)
+    for r in range(1, n):
+        ln_copy(r, me, lax.rem(me + r, n)).start()
+    for r in range(1, n):
+        src = lax.rem(me + n - r, n)
+        ln_copy(r, src, src).wait()
+    grad = d_ln[0]
+    for d in range(1, n):
+        grad = grad + d_ln[d]
+    lnp_o[...], lnm1_o[...], lnm2_o[...] = adam_step(lnp[...], grad, lnm1[...], lnm2[...], 0.0)
+
+
+def backward(n, hidden, ln_params, ln_mom1, ln_mom2, lse, scale, tgt, z, out_embed):
+    tok, dim = hidden.shape
+    vocab = out_embed.shape[0]
     tiles = 3
     vt = vocab // tiles
+    chips = n // 2
     f32, bf16 = jnp.float32, jnp.bfloat16
-    row = pl.BlockSpec((None, 1, tok), lambda b, t: (b, 0, 0))
+    vmem = pl.BlockSpec(memory_space=pltpu.VMEM)
+    hbm = pl.BlockSpec(memory_space=pl.ANY)
+    dma = pltpu.SemaphoreType.DMA
     return pl.pallas_call(
-        dx_kernel,
-        name="dz_dx",
-        grid=(n, tiles),
-        in_specs=[
-            pl.BlockSpec((None, vt, tok), lambda b, t: (b, t, 0)),
-            pl.BlockSpec((vt, dim), lambda b, t: (jnp.where(b == 0, t, tiles - 1), 0)),
-            row, row, row,
+        functools.partial(backward_kernel, n, tiles),
+        name="backward",
+        out_shape=(
+            jax.ShapeDtypeStruct((vocab, n * tok), bf16),
+            jax.ShapeDtypeStruct((tok, dim), bf16),
+            jax.ShapeDtypeStruct((2, dim), f32),
+            jax.ShapeDtypeStruct((2, dim), f32),
+            jax.ShapeDtypeStruct((2, dim), f32),
+        ),
+        in_specs=[vmem] * 7 + [hbm, hbm],
+        out_specs=(hbm, vmem, vmem, vmem, vmem),
+        scratch_shapes=[pltpu.VMEM((vt, tok), f32)] * 3 + [pltpu.VMEM((vt, tok), bf16)] * 3 + [
+            pltpu.VMEM((vocab, dim), bf16),
+            pltpu.VMEM((tiles, dim, vt), bf16),
+            pltpu.VMEM((dim, tok), f32),
+            pltpu.VMEM((2, dim, tok), f32),
+            pltpu.VMEM((chips, dim, tok), f32),
+            pltpu.VMEM((2, dim, tok), f32),
+            pltpu.VMEM((chips - 1, dim, tok), f32),
+            pltpu.VMEM((n, 2, dim), f32),
+            dma((tiles,)), dma((tiles,)), dma((tiles,)),
+            dma((chips,)), dma((chips,)), dma((chips - 1,)), dma((chips - 1,)), dma((n - 1,)), dma((n - 1,)),
         ],
-        out_specs=(
-            pl.BlockSpec((vt, tok), lambda b, t: (t, b)),
-            pl.BlockSpec((None, dim, tok), lambda b, t: (b, 0, 0)),
-        ),
-        out_shape=(jax.ShapeDtypeStruct((vocab, n * tok), bf16), jax.ShapeDtypeStruct((n, dim, tok), f32)),
-        scratch_shapes=[pltpu.VMEM((tiles, dim, vt), bf16)],
-        compiler_params=pltpu.CompilerParams(vmem_limit_bytes=VMEM_LIMIT, dimension_semantics=("arbitrary", "arbitrary")),
+        compiler_params=pltpu.CompilerParams(collective_id=1, has_side_effects=True, vmem_limit_bytes=66_000_000),
         cost_estimate=pl.CostEstimate(flops=2 * n * tok * dim * vocab, bytes_accessed=6 * n * tok * vocab, transcendentals=n * tok * vocab),
-    )(z, out_embed, lse.reshape(n, 1, tok), scale.reshape(n, 1, tok), tgt.reshape(n, 1, tok))
-
-
-def update_kernel(dz, x, e, m, v, e_o, m_o, v_o, grad):
+    )(hidden, ln_params, ln_mom1, ln_mom2, lse, scale, tgt, z, out_embed)
+
+
+def update_kernel(steps, dz, x, e, m, v, e_o, m_o, v_o, grad_a, grad_b):
     i = pl.program_id(0)
-    last = pl.num_programs(0) - 1
-
-    def adam():
-        g = grad[lax.rem(i + 1, 2)]
-        new_e, m_o[...], v_o[...] = adam_step(e[...].astype(jnp.float32), g, m[...], v[...], WEIGHT_DECAY)
-        e_o[...] = new_e.astype(jnp.bfloat16)
-
-    @pl.when(i < last)
+
+    def adam(grad):
+        for lo, size in row_chunks(grad.shape[0], ADAM_ROWS):
+            part = slice(lo, lo + size)
+            new_e, m_o[part, :], v_o[part, :] = adam_step(e[part, :].astype(jnp.float32), grad[part, :], m[part, :], v[part, :], WEIGHT_DECAY)
+            e_o[part, :] = new_e.astype(jnp.bfloat16)
+
+    def both(new, old):
+        adam(old)
+        new[...] = jnp.dot(dz[...], x[...], preferred_element_type=jnp.float32)
+
+    @pl.when((i < steps) & (lax.rem(i, 2) == 0))
     def _():
-        grad[lax.rem(i, 2)] = jnp.dot(dz[...], x[...], preferred_element_type=jnp.float32)
-        adam()
-
-    @pl.when(i == last)
+        both(grad_a, grad_b)
+
+    @pl.when((i < steps) & (lax.rem(i, 2) == 1))
     def _():
-        adam()
+        both(grad_b, grad_a)
+
+    @pl.when(i == steps)
+    def _():
+        adam((grad_a, grad_b)[(steps - 1) % 2])
 
 
 def update(dz, x, out_embed, mom1, mom2):
@@ -412,7 +551,7 @@
     f32, bf16 = jnp.float32, jnp.bfloat16
     late = pl.BlockSpec((vt, dim), lambda i: (jnp.maximum(i - 1, 0), 0))
     return pl.pallas_call(
-        update_kernel,
+        functools.partial(update_kernel, steps),
         name="update",
         grid=(steps + 1,),
         in_specs=[
@@ -422,7 +561,7 @@
         ],
         out_specs=(late, late, late),
         out_shape=(jax.ShapeDtypeStruct((vocab, dim), bf16), jax.ShapeDtypeStruct((vocab, dim), f32), jax.ShapeDtypeStruct((vocab, dim), f32)),
-        scratch_shapes=[pltpu.VMEM((2, vt, dim), f32)],
+        scratch_shapes=[pltpu.VMEM((vt, dim), f32), pltpu.VMEM((vt, dim), f32)],
         compiler_params=pltpu.CompilerParams(vmem_limit_bytes=VMEM_LIMIT, dimension_semantics=("arbitrary",)),
         cost_estimate=pl.CostEstimate(flops=2 * toks * dim * vocab, bytes_accessed=2 * toks * vocab + 20 * vocab * dim, transcendentals=2 * vocab * dim),
     )(dz, x, out_embed, mom1, mom2)
@@ -440,13 +579,8 @@
         tok, dim = hidden.shape
         tm = jnp.stack([targets, loss_mask])
         z, x_full, lse, scale, tgt, loss, mean = forward(n, hidden, tm, ln_params, out_embed)
-        dz, dx = dz_dx(z, out_embed, lse, scale, tgt)
-        d_x_t = lax.psum_scatter(dx, "tp", scatter_dimension=0, tiled=False)
+        dz, d_hidden, ln_new, ln_mom1_new, ln_mom2_new = backward(n, hidden, ln_params, ln_mom1, ln_mom2, lse, scale, tgt, z, out_embed)
         embed_new, embed_mom1_new, embed_mom2_new = update(dz, x_full.reshape(n * tok, dim), out_embed, embed_mom1, embed_mom2)
-        _, ln_vjp = jax.vjp(layer_norm, hidden, ln_params)
-        d_hidden, d_ln = ln_vjp(d_x_t.T)
-        d_ln = lax.psum(d_ln, "tp")
-        ln_new, ln_mom1_new, ln_mom2_new = adam_step(ln_params, d_ln, ln_mom1, ln_mom2, 0.0)
         return (loss.reshape(tok), mean[0, :1], d_hidden, ln_new, ln_mom1_new, ln_mom2_new, embed_new, embed_mom1_new, embed_mom2_new)
 
     return jax.shard_map(device_step, mesh=mesh, in_specs=(row_spec, tok_spec, tok_spec, repl_spec, vocab_spec, repl_spec, repl_spec, vocab_spec, vocab_spec), out_specs=(tok_spec, P("dp"), row_spec, part_spec, part_spec, part_spec, row_spec, row_spec, row_spec), check_vma=False)

time: 257 us -> 244 us (0.949)
  Pallas kernels: 215 us -> 238 us
  between operations: 15.3 us -> 1.89 us
  blocking collectives: 12.4 us -> 0 us
  local copies, waits for them, and re-layouts: 7.54 us -> 3.27 us
  other arithmetic: 5.36 us -> 1.3 us
    pallas_call x2, Pallas kernels: 142 us -> 165 us  [the longest x1 84.9 us: backward(): pl.pallas_call(functools.partial(backward_kernel, n, tiles), name='backwa...]
    psum x1 -> x0, blocking collectives: 12.4 us -> none  [device_step(): d_ln = lax.psum(d_ln, 'tp')]
    reshape x5 -> x0, local copies, waits for them, and re-layouts: 4.01 us -> none  [the longest x1 1.33 us: dz_dx(): lse.reshape(n, 1, tok)]
    reduce_sum x4 -> x0, other arithmetic: 2.93 us -> none  [the longest x1 1.9 us: layer_norm(): row_var = jnp.mean(centered * centered, axis=-1, keepdims=True)]
  transfers between devices with their start and end apart: 1 -> 0, of which waited for: 0 -> 0; matrix products, arithmetic and copies ran while one was open for 0% -> 0% of each run, Pallas kernels for 27% -> 0%
where the time goes in v2:
time: 244 us
  Pallas kernels  238 us (98%)
  local copies, waits for them, and re-layouts  3.27 us (1%)
    pallas_call x1, Pallas kernels, backward(): pl.pallas_call(functools.partial(backward_kernel, n, tiles), name='backwa...  84.9 us
    pallas_call x1, Pallas kernels, update(): pl.pallas_call(functools.partial(update_kernel, steps), name='update', gr...  80.6 us
    pallas_call x1, Pallas kernels, forward(): pl.pallas_call(functools.partial(forward_kernel, n, tiles), name='forward...  72.3 us

profile of v2, /device:TPU:113, one launch (start us, length us, event | category | flops | bytes accessed | tf_op | source)
XLA Modules:
  0.0 244.3 jit_solution(11950982746155324794)
XLA Ops:
  0.6 1.3 pad_add_fusion.tm
  1.9 72.3 %forward.1 = (f32[8,6288,512]{2,1,0:T(8,128)}, bf16[8,512,768]{2,1,0:T(8,128)(2,1)}, f32[8,1,512]{2,1,0:T(1,128)}, f32[8,1,512]{2,1,0:T(1,128)}, s32[8,1,512]{2,...) custom-call(bf16[512,768]{1,0:T(8,128)(2,1)} %hid.3, s32[2,512]{1,0:T(2,128)} %pad_add_fusion.tm, f32[2,768]{1,0:T(2,128)} %lnp.3, ...), custom_call_target="tpu_custom_call" | custom-call | flops 39560675328 | bytes 103022592 | tf_op jit(solution)/shard_map/forward/pallas_call | solution.py:300
  74.3 84.9 %backward.1 = (bf16[6288,4096]{1,0:T(8,128)(2,1)}, bf16[512,768]{1,0:T(8,128)(2,1)}, f32[2,768]{1,0:T(2,128)}, f32[2,768]{1,0:T(2,128)}, f32[2,768]{1,0:T(2,128)}) custom-call(bf16[512,768]{1,0:T(8,128)(2,1)} %hid.3, f32[2,768]{1,0:T(2,128)} %lnp.3, f32[2,768]{1,0:T(2,128)} %lnm1.1, f32[2,768]{1,0:T(2,128)} %lnm2.1, f32[8,1,512]{2,1,0:T(1,128)} %get-tuple-element.26.lse, ...), custom_call_target="tpu_custom_call" | custom-call | flops 39560675328 | bytes 154533888 | tf_op jit(solution)/shard_map/backward/pallas_call | solution.py:491
  159.2 0.0 copy-start.4
  159.3 0.0 copy-start.5
  159.3 0.0 copy-start
  159.3 0.0 copy-start.3
  159.3 0.0 copy-start.2
  159.3 0.0 copy-start.1
  159.3 80.6 %update.1 = (bf16[6288,768]{1,0:T(8,128)(2,1)}, f32[6288,768]{1,0:T(8,128)}, f32[6288,768]{1,0:T(8,128)}) custom-call(bf16[6288,4096]{1,0:T(8,128)(2,1)} %get-tuple-element.34.dz, bf16[4096,768]{1,0:T(8,128)(2,1)} %bitcast.9, bf16[6288,768]{1,0:T(8,128)(2,1)} %e.1, f32[6288,768]{1,0:T(8,128)} %m.1, f32[6288,768]{1,0:T(8,128)} %v.1), custom_call_target="tpu_custom_call" | custom-call | flops 39560675328 | bytes 148094976 | tf_op jit(solution)/shard_map/update/pallas_call | solution.py:553
  239.9 0.0 copy-done.4
  239.9 0.6 copy.24
  240.4 0.0 copy-done.5
  240.5 0.0 copy-done
  240.5 0.9 copy.26
  241.4 0.0 copy-done.3
  241.4 0.6 copy.27
  242.0 0.0 copy-done.2
  242.0 0.6 copy.28
  242.6 0.0 copy-done.1
  242.6 0.6 copy.29
Async XLA Ops:
  159.2 80.6 %copy-start.4 = (f32[1,512]{1,0:T(1,128)S(1)}, f32[1,512]{1,0:T(1,128)}, u32[]{:S(2)}) copy-start(f32[1,512]{1,0:T(1,128)} %get-tuple-element.24) | copy-start | bytes 6148
  159.3 81.2 %copy-start.5 = (f32[1,128]{1,0:T(1,128)S(1)}, f32[1,128]{1,0:T(1,128)}, u32[]{:S(2)}) copy-start(f32[1,128]{1,0:T(1,128)} %get-tuple-element.25) | copy-start | bytes 1540
  159.3 81.2 %copy-start = (bf16[512,768]{1,0:T(8,128)(2,1)S(1)}, bf16[512,768]{1,0:T(8,128)(2,1)}, u32[]{:S(2)}) copy-start(bf16[512,768]{1,0:T(8,128)(2,1)} %get-tuple-element.50) | copy-start | bytes 2359300
  159.3 82.1 %copy-start.3 = (f32[2,768]{1,0:T(2,128)S(1)}, f32[2,768]{1,0:T(2,128)}, u32[]{:S(2)}) copy-start(f32[2,768]{1,0:T(2,128)} %get-tuple-element.51) | copy-start | bytes 18436
  159.3 82.7 %copy-start.2 = (f32[2,768]{1,0:T(2,128)S(1)}, f32[2,768]{1,0:T(2,128)}, u32[]{:S(2)}) copy-start(f32[2,768]{1,0:T(2,128)} %get-tuple-element.52) | copy-start | bytes 18436
  159.3 83.3 %copy-start.1 = (f32[2,768]{1,0:T(2,128)S(1)}, f32[2,768]{1,0:T(2,128)}, u32[]{:S(2)}) copy-start(f32[2,768]{1,0:T(2,128)} %get-tuple-element.53) | copy-start | bytes 18436

commit v3 on v1

--- a/solution.py
+++ b/solution.py
@@ -19,6 +19,8 @@
 VMEM_LIMIT = 64_000_000
 NEG = -3.0e38
 STAT_ROWS = 64
+ADAM_ROWS = 16
+DZ_ROWS = 64
 DOT_ROWS = 1056
 
 
@@ -34,9 +36,9 @@
 def adam_step(param_val, grad_val, m_old, v_old, decay_rate):
     m_new = BETA_ONE * m_old + (1.0 - BETA_ONE) * grad_val
     v_new = BETA_TWO * v_old + (1.0 - BETA_TWO) * grad_val * grad_val
-    m_hat = m_new / (1.0 - BETA_ONE ** ADAM_STEP)
-    v_hat = v_new / (1.0 - BETA_TWO ** ADAM_STEP)
-    new_param = param_val - LEARN_RATE * (m_hat / (jnp.sqrt(v_hat) + ADAM_EPS) + decay_rate * param_val)
+    m_step = m_new * (LEARN_RATE / (1.0 - BETA_ONE ** ADAM_STEP))
+    v_hat = v_new * (1.0 / (1.0 - BETA_TWO ** ADAM_STEP))
+    new_param = (1.0 - LEARN_RATE * decay_rate) * param_val - m_step / (jnp.sqrt(v_hat) + ADAM_EPS)
     return new_param, m_new, v_new
 
 
@@ -256,8 +258,6 @@
     z_copy(total - 2, z_a).wait()
     send_stats(n - 1)
     z_copy(total - 1, z_b).wait()
-    for c in (s0, s2, s3, s4, s5, s6):
-        pass
     s0.wait_send()
     s3.wait_send()
     s4.wait_send()
@@ -280,9 +280,13 @@
     mask = tm_full[:, 1, :].astype(jnp.float32)
     count = jnp.sum(mask)
     loss = (lse - tgt_logit) * mask
-    lse_o[...] = lse
-    scale_o[...] = mask / count
-    tgt_o[...] = tm_full[:, 0, :] - me * vocab
+    half = tok // 2
+    for d in range(n):
+        for h in range(2):
+            part = slice(h * half, (h + 1) * half)
+            lse_o[2 * d + h] = lse[d:d + 1, part]
+            scale_o[2 * d + h] = mask[d:d + 1, part] / count
+            tgt_o[2 * d + h] = tm_full[d, 0:1, part] - me * vocab
     own = lax.broadcasted_iota(jnp.int32, loss.shape, 0) == me
     loss_o[...] = jnp.sum(jnp.where(own, loss, 0.0), axis=0, keepdims=True)
     mean_o[...] = jnp.full(mean_o.shape, jnp.sum(loss) / count, jnp.float32)
@@ -303,9 +307,9 @@
         out_shape=(
             jax.ShapeDtypeStruct((n, vocab, tok), f32),
             jax.ShapeDtypeStruct((n, tok, dim), bf16),
-            jax.ShapeDtypeStruct((n, tok), f32),
-            jax.ShapeDtypeStruct((n, tok), f32),
-            jax.ShapeDtypeStruct((n, tok), i32),
+            jax.ShapeDtypeStruct((2 * n, 1, tok // 2), f32),
+            jax.ShapeDtypeStruct((2 * n, 1, tok // 2), f32),
+            jax.ShapeDtypeStruct((2 * n, 1, tok // 2), i32),
             jax.ShapeDtypeStruct((1, tok), f32),
             jax.ShapeDtypeStruct((1, 128), f32),
         ),
@@ -333,96 +337,222 @@
     )(hidden, tm, ln_params, out_embed)
 
 
-def dx_kernel(z, e, lse, scale, tgt, dz_o, dx_o, e_t):
-    b, t = pl.program_id(0), pl.program_id(1)
-    vt, tok = z.shape
-
-    @pl.when(b == 0)
-    def _():
-        e_t[t] = e[...].T
-
-    l, sc = lse[...], scale[...]
-    want = tgt[...] - t * vt
-    for lo, size in row_chunks(vt, 128):
-        rows = lax.broadcasted_iota(jnp.int32, (size, tok), 0) + lo
-        hot = jnp.where(rows == want, 1.0, 0.0)
-        dz_o[lo:lo + size, :] = ((jnp.exp(z[lo:lo + size, :] - l) - hot) * sc).astype(jnp.bfloat16)
-    part = jnp.dot(e_t[t], dz_o[...], preferred_element_type=jnp.float32)
-
-    @pl.when(t == 0)
-    def _():
-        dx_o[...] = part
-
-    @pl.when(t > 0)
-    def _():
-        dx_o[...] += part
-
-
-def dz_dx(z, out_embed, lse, scale, tgt):
-    n, vocab, tok = z.shape
-    dim = out_embed.shape[1]
-    tiles = 3
-    vt = vocab // tiles
+def vocab_parts(vocab):
+    size = vocab // 3 // 256 * 256
+    return [(0, size), (size, size), (2 * size, vocab - 2 * size)]
+
+
+def backward_kernel(n, hid, lnp, lse, scale, tgt, z_hbm, e_hbm,
+                    dz_hbm, dh_o, dln_o,
+                    z_0, z_1, z_2, dz_0, dz_1, dz_2, e_in, e_t, acc, own_part, to_pair, from_pair, to_ring, from_ring, d_ln,
+                    z_sem, dz_sem, e_sem, pair_send, pair_recv, ring_send, ring_recv, ln_send, ln_recv):
+    me = lax.axis_index("tp")
+    chips = n // 2
+    chip, core = me // 2, lax.rem(me, 2)
+    sgn = 1 - 2 * core
+    vocab, half = e_in.shape[0], acc.shape[1] // 2
+    z_bufs, dz_bufs = (z_0, z_1, z_2), (dz_0, dz_1, dz_2)
+    parts = vocab_parts(vocab)
+    rounds = 2 * chips
+
+    def dev(chip_idx, core_idx):
+        return lax.rem(chip_idx + 2 * chips, chips) * 2 + core_idx
+
+    partner = dev(chip, 1 - core)
+    ahead = dev(chip + sgn, core)
+
+    def block_of(u, own):
+        hop = 1 + u // 2
+        return dev(chip - sgn * hop, core) if own else dev(chip + sgn * hop, 1 - core)
+
+    def z_copies(u, t):
+        lo, size = parts[t]
+        cols = pl.ds(pl.multiple_of(lax.rem(u, 2) * half, half), half)
+        return [pltpu.make_async_copy(z_hbm.at[block_of(u, own), pl.ds(lo, size), cols], z_bufs[t].at[:, own * half:(own + 1) * half], z_sem.at[t, own])
+                for own in range(2)]
+
+    def dz_copies(u, t):
+        lo, size = parts[t]
+        cols = [pl.ds(pl.multiple_of((block_of(u, own) * 2 + lax.rem(u, 2)) * half, half), half) for own in range(2)]
+        return [pltpu.make_async_copy(dz_bufs[t].at[:, own * half:(own + 1) * half], dz_hbm.at[pl.ds(lo, size), cols[own]], dz_sem.at[t, own])
+                for own in range(2)]
+
+    def start(copies):
+        for c in copies:
+            c.start()
+
+    def wait(copies):
+        for c in copies:
+            c.wait()
+
+    e_copies = [pltpu.make_async_copy(e_hbm.at[pl.ds(lo, size)], e_in.at[pl.ds(lo, size)], e_sem.at[k]) for k, (lo, size) in enumerate(parts)]
+    start(e_copies)
+    for t in range(len(parts)):
+        start(z_copies(0, t))
+
+    barrier = pltpu.get_barrier_semaphore()
+    for r in range(1, n):
+        pl.semaphore_signal(barrier, inc=1, device_id={"tp": lax.rem(me + r, n)}, device_id_type=MESH)
+    for c, (lo, size) in zip(e_copies, parts):
+        c.wait()
+        e_t[:, lo:lo + size] = e_in[lo:lo + size, :].T
+    pl.semaphore_wait(barrier, n - 1)
+
+    def pair_copy(u):
+        return pltpu.make_async_remote_copy(src_ref=to_pair.at[lax.rem(u, 2)], dst_ref=from_pair.at[u], send_sem=pair_send.at[u],
+                                            recv_sem=pair_recv.at[u], device_id={"tp": partner}, device_id_type=MESH)
+
+    def ring_copy(u):
+        return pltpu.make_async_remote_copy(src_ref=to_ring.at[lax.rem(u, 2)], dst_ref=from_ring.at[u], send_sem=ring_send.at[u],
+                                            recv_sem=ring_recv.at[u], device_id={"tp": ahead}, device_id_type=MESH)
+
+    def combine(u):
+        slot = lax.rem(u, 2)
+        pair_copy(u).wait_recv()
+
+        @pl.when(u < 2)
+        def _():
+            to_ring[slot] = own_part[slot] + from_pair[u]
+            ring_copy(u).start()
+
+        @pl.when((u >= 2) & (u < rounds - 2))
+        def _():
+            ring_copy(u - 2).wait()
+            to_ring[slot] = own_part[slot] + from_pair[u] + from_ring[u - 2]
+            ring_copy(u).start()
+
+        @pl.when(u >= rounds - 2)
+        def _():
+            ring_copy(u - 2).wait()
+            to_ring[slot] = own_part[slot] + from_pair[u] + from_ring[u - 2]
+
+    def body(u, carry):
+        slot = lax.rem(u, 2)
+        both = [block_of(u, own) * 2 + slot for own in range(2)]
+        l, sc, want = (jnp.concatenate([ref[both[0]], ref[both[1]]], axis=1) for ref in (lse, scale, tgt))
+        for t, (first, count) in enumerate(parts):
+            z, dz = z_bufs[t], dz_bufs[t]
+
+            @pl.when(u > 0)
+            def _():
+                wait(dz_copies(u - 1, t))
+
+            wait(z_copies(u, t))
+            seek = want - first
+            for lo, size in row_chunks(count, DZ_ROWS):
+                rows = lax.broadcasted_iota(jnp.int32, (size, 2 * half), 0) + lo
+                hot = jnp.where(rows == seek, 1.0, 0.0)
+                dz[lo:lo + size, :] = ((jnp.exp(z[lo:lo + size, :] - l) - hot) * sc).astype(jnp.bfloat16)
+            part = jnp.dot(e_t[:, first:first + count], dz[...], preferred_element_type=jnp.float32)
+            acc[...] = part if t == 0 else acc[...] + part
+            start(dz_copies(u, t))
+
+            @pl.when(u < rounds - 1)
+            def _():
+                start(z_copies(u + 1, t))
+
+        @pl.when(u > 0)
+        def _():
+            combine(u - 1)
+
+        @pl.when(u >= 2)
+        def _():
+            pair_copy(u - 2).wait_send()
+        to_pair[slot] = acc[:, :half]
+        own_part[slot] = acc[:, half:]
+        pair_copy(u).start()
+        return carry
+
+    lax.fori_loop(0, rounds, body, 0)
+    combine(rounds - 1)
+    for u in (rounds - 2, rounds - 1):
+        pair_copy(u).wait_send()
+    for t in range(len(parts)):
+        wait(dz_copies(rounds - 1, t))
+
+    d_x = jnp.concatenate([to_ring[0].T, to_ring[1].T], axis=0)
+    rows = hid[...].astype(jnp.float32)
+    centered = rows - jnp.mean(rows, axis=-1, keepdims=True)
+    rstd = lax.rsqrt(jnp.mean(centered * centered, axis=-1, keepdims=True) + LN_EPS)
+    normed = centered * rstd
+    d_ln[me] = jnp.concatenate([jnp.sum(d_x * normed, axis=0, keepdims=True), jnp.sum(d_x, axis=0, keepdims=True)], axis=0)
+
+    def ln_copy(r, slot, peer):
+        return pltpu.make_async_remote_copy(src_ref=d_ln.at[slot], dst_ref=d_ln.at[slot], send_sem=ln_send.at[r - 1],
+                                            recv_sem=ln_recv.at[r - 1], device_id={"tp": peer}, device_id_type=MESH)
+
+    d_normed = d_x * lnp[0:1, :]
+    proj = jnp.mean(d_normed * normed, axis=-1, keepdims=True)
+    dh_o[...] = (rstd * (d_normed - jnp.mean(d_normed, axis=-1, keepdims=True) - normed * proj)).astype(jnp.bfloat16)
+    for r in range(1, n):
+        ln_copy(r, me, lax.rem(me + r, n)).start()
+    for r in range(1, n):
+        src = lax.rem(me + n - r, n)
+        ln_copy(r, src, src).wait()
+    grad = d_ln[0]
+    for d in range(1, n):
+        grad = grad + d_ln[d]
+    dln_o[...] = grad
+
+
+def backward(n, hidden, ln_params, lse, scale, tgt, z, out_embed):
+    tok, dim = hidden.shape
+    vocab = out_embed.shape[0]
+    half = tok // 2
     f32, bf16 = jnp.float32, jnp.bfloat16
-    row = pl.BlockSpec((None, 1, tok), lambda b, t: (b, 0, 0))
+    vmem = pl.BlockSpec(memory_space=pltpu.VMEM)
+    hbm = pl.BlockSpec(memory_space=pl.ANY)
+    dma = pltpu.SemaphoreType.DMA
     return pl.pallas_call(
-        dx_kernel,
-        name="dz_dx",
-        grid=(n, tiles),
-        in_specs=[
-            pl.BlockSpec((None, vt, tok), lambda b, t: (b, t, 0)),
-            pl.BlockSpec((vt, dim), lambda b, t: (jnp.where(b == 0, t, tiles - 1), 0)),
-            row, row, row,
+        functools.partial(backward_kernel, n),
+        name="backward",
+        out_shape=(
+            jax.ShapeDtypeStruct((vocab, n * tok), bf16),
+            jax.ShapeDtypeStruct((tok, dim), bf16),
+            jax.ShapeDtypeStruct((2, dim), f32),
+        ),
+        in_specs=[vmem] * 5 + [hbm, hbm],
+        out_specs=(hbm, vmem, vmem),
+        scratch_shapes=[pltpu.VMEM((size, tok), f32) for _, size in vocab_parts(vocab)] + [pltpu.VMEM((size, tok), bf16) for _, size in vocab_parts(vocab)] + [
+            pltpu.VMEM((vocab, dim), bf16),
+            pltpu.VMEM((dim, vocab), bf16),
+            pltpu.VMEM((dim, tok), f32),
+            pltpu.VMEM((2, dim, half), f32),
+            pltpu.VMEM((2, dim, half), f32),
+            pltpu.VMEM((n, dim, half), f32),
+            pltpu.VMEM((2, dim, half), f32),
+            pltpu.VMEM((n - 2, dim, half), f32),
+            pltpu.VMEM((n, 2, dim), f32),
+            dma((3, 2)), dma((3, 2)), dma((3,)),
+            dma((n,)), dma((n,)), dma((n - 2,)), dma((n - 2,)), dma((n - 1,)), dma((n - 1,)),
         ],
-        out_specs=(
-            pl.BlockSpec((vt, tok), lambda b, t: (t, b)),
-            pl.BlockSpec((None, dim, tok), lambda b, t: (b, 0, 0)),
-        ),
-        out_shape=(jax.ShapeDtypeStruct((vocab, n * tok), bf16), jax.ShapeDtypeStruct((n, dim, tok), f32)),
-        scratch_shapes=[pltpu.VMEM((tiles, dim, vt), bf16)],
-        compiler_params=pltpu.CompilerParams(vmem_limit_bytes=VMEM_LIMIT, dimension_semantics=("arbitrary", "arbitrary")),
+        compiler_params=pltpu.CompilerParams(collective_id=1, has_side_effects=True, vmem_limit_bytes=66_000_000),
         cost_estimate=pl.CostEstimate(flops=2 * n * tok * dim * vocab, bytes_accessed=6 * n * tok * vocab, transcendentals=n * tok * vocab),
-    )(z, out_embed, lse.reshape(n, 1, tok), scale.reshape(n, 1, tok), tgt.reshape(n, 1, tok))
+    )(hidden, ln_params, lse, scale, tgt, z, out_embed)
 
 
 def update_kernel(dz, x, e, m, v, e_o, m_o, v_o, grad):
-    i = pl.program_id(0)
-    last = pl.num_programs(0) - 1
-
-    def adam():
-        g = grad[lax.rem(i + 1, 2)]
-        new_e, m_o[...], v_o[...] = adam_step(e[...].astype(jnp.float32), g, m[...], v[...], WEIGHT_DECAY)
-        e_o[...] = new_e.astype(jnp.bfloat16)
-
-    @pl.when(i < last)
-    def _():
-        grad[lax.rem(i, 2)] = jnp.dot(dz[...], x[...], preferred_element_type=jnp.float32)
-        adam()
-
-    @pl.when(i == last)
-    def _():
-        adam()
+    grad[...] = jnp.dot(dz[...], x[...], preferred_element_type=jnp.float32)
+    for lo, size in row_chunks(grad.shape[0], ADAM_ROWS):
+        part = slice(lo, lo + size)
+        new_e, m_o[part, :], v_o[part, :] = adam_step(e[part, :].astype(jnp.float32), grad[part, :], m[part, :], v[part, :], WEIGHT_DECAY)
+        e_o[part, :] = new_e.astype(jnp.bfloat16)
 
 
 def update(dz, x, out_embed, mom1, mom2):
     vocab, dim = out_embed.shape
     toks = x.shape[0]
     vt = 640
-    steps = pl.cdiv(vocab, vt)
     f32, bf16 = jnp.float32, jnp.bfloat16
-    late = pl.BlockSpec((vt, dim), lambda i: (jnp.maximum(i - 1, 0), 0))
+    tile = pl.BlockSpec((vt, dim), lambda i: (i, 0))
     return pl.pallas_call(
         update_kernel,
         name="update",
-        grid=(steps + 1,),
-        in_specs=[
-            pl.BlockSpec((vt, toks), lambda i: (jnp.minimum(i, steps - 1), 0)),
-            pl.BlockSpec((toks, dim), lambda i: (0, 0)),
-            late, late, late,
-        ],
-        out_specs=(late, late, late),
+        grid=(pl.cdiv(vocab, vt),),
+        in_specs=[pl.BlockSpec((vt, toks), lambda i: (i, 0)), pl.BlockSpec((toks, dim), lambda i: (0, 0)), tile, tile, tile],
+        out_specs=(tile, tile, tile),
         out_shape=(jax.ShapeDtypeStruct((vocab, dim), bf16), jax.ShapeDtypeStruct((vocab, dim), f32), jax.ShapeDtypeStruct((vocab, dim), f32)),
-        scratch_shapes=[pltpu.VMEM((2, vt, dim), f32)],
+        scratch_shapes=[pltpu.VMEM((vt, dim), f32)],
         compiler_params=pltpu.CompilerParams(vmem_limit_bytes=VMEM_LIMIT, dimension_semantics=("arbitrary",)),
         cost_estimate=pl.CostEstimate(flops=2 * toks * dim * vocab, bytes_accessed=2 * toks * vocab + 20 * vocab * dim, transcendentals=2 * vocab * dim),
     )(dz, x, out_embed, mom1, mom2)
@@ -440,13 +570,9 @@
         tok, dim = hidden.shape
         tm = jnp.stack([targets, loss_mask])
         z, x_full, lse, scale, tgt, loss, mean = forward(n, hidden, tm, ln_params, out_embed)
-        dz, dx = dz_dx(z, out_embed, lse, scale, tgt)
-        d_x_t = lax.psum_scatter(dx, "tp", scatter_dimension=0, tiled=False)
+        dz, d_hidden, d_ln = backward(n, hidden, ln_params, lse, scale, tgt, z, out_embed)
+        ln_new, ln_mom1_new, ln_mom2_new = adam_step(ln_params, d_ln, ln_mom1, ln_mom2, 0.0)
         embed_new, embed_mom1_new, embed_mom2_new = update(dz, x_full.reshape(n * tok, dim), out_embed, embed_mom1, embed_mom2)
-        _, ln_vjp = jax.vjp(layer_norm, hidden, ln_params)
-        d_hidden, d_ln = ln_vjp(d_x_t.T)
-        d_ln = lax.psum(d_ln, "tp")
-        ln_new, ln_mom1_new, ln_mom2_new = adam_step(ln_params, d_ln, ln_mom1, ln_mom2, 0.0)
         return (loss.reshape(tok), mean[0, :1], d_hidden, ln_new, ln_mom1_new, ln_mom2_new, embed_new, embed_mom1_new, embed_mom2_new)
 
     return jax.shard_map(device_step, mesh=mesh, in_specs=(row_spec, tok_spec, tok_spec, repl_spec, vocab_spec, repl_spec, repl_spec, vocab_spec, vocab_spec), out_specs=(tok_spec, P("dp"), row_spec, part_spec, part_spec, part_spec, row_spec, row_spec, row_spec), check_vma=False)

time: 257 us -> 222 us (0.86)
  between operations: 15.3 us -> 1.89 us
  blocking collectives: 12.4 us -> 0 us
  local copies, waits for them, and re-layouts: 7.54 us -> 1.49 us
  other arithmetic: 5.36 us -> 2.61 us
    psum x1 -> x0, blocking collectives: 12.4 us -> none  [device_step(): d_ln = lax.psum(d_ln, 'tp')]
    reshape x5 -> x0, local copies, waits for them, and re-layouts: 4.01 us -> none  [the longest x1 1.33 us: dz_dx(): lse.reshape(n, 1, tok)]
    reduce_sum x4 -> x0, other arithmetic: 2.93 us -> none  [the longest x1 1.9 us: layer_norm(): row_var = jnp.mean(centered * centered, axis=-1, keepdims=True)]
  transfers between devices with their start and end apart: 1 -> 0, of which waited for: 0 -> 0; matrix products, arithmetic and copies ran while one was open for 0% -> 0% of each run, Pallas kernels for 27% -> 0%
where the time goes in v3:
time: 222 us
  Pallas kernels  216 us (97%)
  other arithmetic  2.61 us (1%)
    pallas_call x1, Pallas kernels, backward(): pl.pallas_call(functools.partial(backward_kernel, n), name='backward', ou...  80.7 us
    pallas_call x1, Pallas kernels, forward(): pl.pallas_call(functools.partial(forward_kernel, n, tiles), name='forward...  72.4 us
    pallas_call x1, Pallas kernels, update(): pl.pallas_call(update_kernel, name='update', grid=(pl.cdiv(vocab, vt),),...  63.1 us

profile of v3, /device:TPU:113, one launch (start us, length us, event | category | flops | bytes accessed | tf_op | source)
XLA Modules:
  0.0 222.2 jit_solution(5431725059186961087)
XLA Ops:
  0.6 1.3 pad_add_fusion.tm
  1.9 72.4 %forward.1 = (f32[8,6288,512]{2,1,0:T(8,128)}, bf16[8,512,768]{2,1,0:T(8,128)(2,1)}, f32[16,1,256]{2,1,0:T(1,128)}, f32[16,1,256]{2,1,0:T(1,128)}, s32[16,1,256]...) custom-call(bf16[512,768]{1,0:T(8,128)(2,1)} %hid.3, s32[2,512]{1,0:T(2,128)} %pad_add_fusion.tm, f32[2,768]{1,0:T(2,128)} %lnp.3, ...), custom_call_target="tpu_custom_call" | custom-call | flops 39560675328 | bytes 103022592 | tf_op jit(solution)/shard_map/forward/pallas_call | solution.py:304
  74.4 0.0 copy-start.1
  74.4 0.0 copy-start.2
  74.4 0.0 copy-start.3
  74.4 80.7 %backward.1 = (bf16[6288,4096]{1,0:T(8,128)(2,1)}, bf16[512,768]{1,0:T(8,128)(2,1)}, f32[2,768]{1,0:T(2,128)}) custom-call(bf16[512,768]{1,0:T(8,128)(2,1)} %hid.3, f32[2,768]{1,0:T(2,128)} %lnp.3, f32[16,1,256]{2,1,0:T(1,128)} %get-tuple-element.24.lse, f32[16,1,256]{2,1,0:T(1,128)} %get-tuple-element.25.scale, s32[16,1,256]{2,1,0:T(1,128)} %get-tuple-element.26.tgt, ...), custom_call_target="tpu_custom_call" | custom-call | flops 39560675328 | bytes 154533888 | tf_op jit(solution)/shard_map/backward/pallas_call | solution.py:506
  155.1 0.0 copy-done.1
  155.1 0.0 copy-done.2
  155.1 0.0 copy-done.3
  155.1 1.3 divide_subtract_fusion
  156.4 0.0 copy-start.4
  156.4 0.0 copy-start.5
  156.4 0.0 copy-start
  156.4 63.1 %update.1 = (bf16[6288,768]{1,0:T(8,128)(2,1)}, f32[6288,768]{1,0:T(8,128)}, f32[6288,768]{1,0:T(8,128)}) custom-call(bf16[6288,4096]{1,0:T(8,128)(2,1)} %get-tuple-element.30.dz, bf16[4096,768]{1,0:T(8,128)(2,1)} %bitcast.9, bf16[6288,768]{1,0:T(8,128)(2,1)} %e.1, f32[6288,768]{1,0:T(8,128)} %m.1, f32[6288,768]{1,0:T(8,128)} %v.1), custom_call_target="tpu_custom_call" | custom-call | flops 39560675328 | bytes 148094976 | tf_op jit(solution)/shard_map/update/pallas_call | solution.py:548
  219.5 0.0 copy-done.4
  219.5 0.6 copy.21
  220.1 0.0 copy-done.5
  220.2 0.0 copy-done
  220.2 0.9 copy.23
Async XLA Ops:
  74.4 80.7 %copy-start.1 = (f32[2,768]{1,0:T(2,128)S(1)}, f32[2,768]{1,0:T(2,128)}, u32[]{:S(2)}) copy-start(f32[2,768]{1,0:T(2,128)} %lnp.3) | copy-start | bytes 18436
  74.4 80.7 %copy-start.2 = (f32[2,768]{1,0:T(2,128)S(1)}, f32[2,768]{1,0:T(2,128)}, u32[]{:S(2)}) copy-start(f32[2,768]{1,0:T(2,128)} %param.14) | copy-start | bytes 18436
  74.4 80.7 %copy-start.3 = (f32[2,768]{1,0:T(2,128)S(1)}, f32[2,768]{1,0:T(2,128)}, u32[]{:S(2)}) copy-start(f32[2,768]{1,0:T(2,128)} %param.15) | copy-start | bytes 18436
  156.4 63.1 %copy-start.4 = (f32[1,512]{1,0:T(1,128)S(1)}, f32[1,512]{1,0:T(1,128)}, u32[]{:S(2)}) copy-start(f32[1,512]{1,0:T(1,128)} %get-tuple-element.22) | copy-start | bytes 6148
  156.4 63.7 %copy-start.5 = (f32[1,128]{1,0:T(1,128)S(1)}, f32[1,128]{1,0:T(1,128)}, u32[]{:S(2)}) copy-start(f32[1,128]{1,0:T(1,128)} %get-tuple-element.23) | copy-start | bytes 1540
  156.4 63.8 %copy-start = (bf16[512,768]{1,0:T(8,128)(2,1)S(1)}, bf16[512,768]{1,0:T(8,128)(2,1)}, u32[]{:S(2)}) copy-start(bf16[512,768]{1,0:T(8,128)(2,1)} %get-tuple-element.49) | copy-start | bytes 2359300

commit v4 on v3

--- a/solution.py
+++ b/solution.py
@@ -116,7 +116,7 @@
     def z_copy(nn, buf):
         p, t = nn // tiles, lax.rem(nn, tiles)
         slot = lax.rem(nn, 2)
-        return pltpu.make_async_copy(buf, z_hbm.at[block_of(p), pl.ds(pl.multiple_of(t * vt, 16), vt)], z_sem.at[slot])
+        return pltpu.make_async_copy(buf, z_hbm.at[pl.ds(2 * block_of(p), 2), pl.ds(pl.multiple_of(t * vt, 16), vt)], z_sem.at[slot])
 
     def x_out(p):
         b = block_of(p)
@@ -139,7 +139,8 @@
     def sums_rows(acc, buf, start, count):
         want, m, s, tgt = acc
         for lo, size in row_chunks(count, STAT_ROWS):
-            z = buf[start + lo:start + lo + size, :].reshape(size // 8, 8, tok)
+            part = slice(start + lo, start + lo + size)
+            z = jnp.concatenate([buf[0, part, :], buf[1, part, :]], axis=1).reshape(size // 8, 8, tok)
             s = s + jnp.sum(jnp.exp(z - m[None]), axis=0)
             rows = lax.broadcasted_iota(jnp.int32, z.shape, 0) * 8 + (start + lo)
             tgt = tgt + jnp.sum(jnp.where(want[None] == rows, z, 0.0), axis=0)
@@ -227,7 +228,8 @@
         acc = sums_begin(jnp.maximum(nn - 1, 0))
         for lo, size in row_chunks(vt, DOT_ROWS):
             z = jnp.dot(e_v[pl.ds(pl.multiple_of(t * vt + lo, 16), size), :], x_t[...], preferred_element_type=jnp.float32)
-            cur[lo:lo + size, :] = z
+            cur[0, lo:lo + size, :] = z[:, :tok // 2]
+            cur[1, lo:lo + size, :] = z[:, tok // 2:]
             top = jnp.maximum(top, jnp.max(z.reshape(size // 8, 8, tok), axis=0))
             acc = sums_rows(acc, prev, lo, size)
         sums_end(acc)
@@ -305,7 +307,7 @@
         functools.partial(forward_kernel, n, tiles),
         name="forward",
         out_shape=(
-            jax.ShapeDtypeStruct((n, vocab, tok), f32),
+            jax.ShapeDtypeStruct((2 * n, vocab, tok // 2), f32),
             jax.ShapeDtypeStruct((n, tok, dim), bf16),
             jax.ShapeDtypeStruct((2 * n, 1, tok // 2), f32),
             jax.ShapeDtypeStruct((2 * n, 1, tok // 2), f32),
@@ -321,8 +323,8 @@
             pltpu.VMEM((n, 2, tok), i32),
             pltpu.VMEM((vocab, dim), bf16),
             pltpu.VMEM((dim, tok), bf16),
-            pltpu.VMEM((vt, tok), f32),
-            pltpu.VMEM((vt, tok), f32),
+            pltpu.VMEM((2, vt, tok // 2), f32),
+            pltpu.VMEM((2, vt, tok // 2), f32),
             pltpu.VMEM((8, tok), f32),
             pltpu.VMEM((8, tok), f32),
             pltpu.VMEM((8, tok), f32),
@@ -367,14 +369,12 @@
 
     def z_copies(u, t):
         lo, size = parts[t]
-        cols = pl.ds(pl.multiple_of(lax.rem(u, 2) * half, half), half)
-        return [pltpu.make_async_copy(z_hbm.at[block_of(u, own), pl.ds(lo, size), cols], z_bufs[t].at[:, own * half:(own + 1) * half], z_sem.at[t, own])
+        return [pltpu.make_async_copy(z_hbm.at[block_of(u, own) * 2 + lax.rem(u, 2), pl.ds(lo, size)], z_bufs[t].at[own], z_sem.at[t, own])
                 for own in range(2)]
 
     def dz_copies(u, t):
         lo, size = parts[t]
-        cols = [pl.ds(pl.multiple_of((block_of(u, own) * 2 + lax.rem(u, 2)) * half, half), half) for own in range(2)]
-        return [pltpu.make_async_copy(dz_bufs[t].at[:, own * half:(own + 1) * half], dz_hbm.at[pl.ds(lo, size), cols[own]], dz_sem.at[t, own])
+        return [pltpu.make_async_copy(dz_bufs[t].at[own], dz_hbm.at[block_of(u, own) * 2 + lax.rem(u, 2), pl.ds(lo, size)], dz_sem.at[t, own])
                 for own in range(2)]
 
     def start(copies):
@@ -429,7 +429,7 @@
     def body(u, carry):
         slot = lax.rem(u, 2)
         both = [block_of(u, own) * 2 + slot for own in range(2)]
-        l, sc, want = (jnp.concatenate([ref[both[0]], ref[both[1]]], axis=1) for ref in (lse, scale, tgt))
+        stats = [(lse[row], scale[row], tgt[row]) for row in both]
         for t, (first, count) in enumerate(parts):
             z, dz = z_bufs[t], dz_bufs[t]
 
@@ -438,12 +438,13 @@
                 wait(dz_copies(u - 1, t))
 
             wait(z_copies(u, t))
-            seek = want - first
             for lo, size in row_chunks(count, DZ_ROWS):
-                rows = lax.broadcasted_iota(jnp.int32, (size, 2 * half), 0) + lo
-                hot = jnp.where(rows == seek, 1.0, 0.0)
-                dz[lo:lo + size, :] = ((jnp.exp(z[lo:lo + size, :] - l) - hot) * sc).astype(jnp.bfloat16)
-            part = jnp.dot(e_t[:, first:first + count], dz[...], preferred_element_type=jnp.float32)
+                rows = lax.broadcasted_iota(jnp.int32, (size, half), 0) + lo
+                for own, (l, sc, want) in enumerate(stats):
+                    hot = jnp.where(rows == want - first, 1.0, 0.0)
+                    dz[own, lo:lo + size, :] = ((jnp.exp(z[own, lo:lo + size, :] - l) - hot) * sc).astype(jnp.bfloat16)
+            both_dz = jnp.concatenate([dz[0], dz[1]], axis=1)
+            part = jnp.dot(e_t[:, first:first + count], both_dz, preferred_element_type=jnp.float32)
             acc[...] = part if t == 0 else acc[...] + part
             start(dz_copies(u, t))
 
@@ -507,13 +508,13 @@
         functools.partial(backward_kernel, n),
         name="backward",
         out_shape=(
-            jax.ShapeDtypeStruct((vocab, n * tok), bf16),
+            jax.ShapeDtypeStruct((2 * n, vocab, half), bf16),
             jax.ShapeDtypeStruct((tok, dim), bf16),
             jax.ShapeDtypeStruct((2, dim), f32),
         ),
         in_specs=[vmem] * 5 + [hbm, hbm],
         out_specs=(hbm, vmem, vmem),
-        scratch_shapes=[pltpu.VMEM((size, tok), f32) for _, size in vocab_parts(vocab)] + [pltpu.VMEM((size, tok), bf16) for _, size in vocab_parts(vocab)] + [
+        scratch_shapes=[pltpu.VMEM((2, size, half), f32) for _, size in vocab_parts(vocab)] + [pltpu.VMEM((2, size, half), bf16) for _, size in vocab_parts(vocab)] + [
             pltpu.VMEM((vocab, dim), bf16),
             pltpu.VMEM((dim, vocab), bf16),
             pltpu.VMEM((dim, tok), f32),
@@ -532,7 +533,8 @@
 
 
 def update_kernel(dz, x, e, m, v, e_o, m_o, v_o, grad):
-    grad[...] = jnp.dot(dz[...], x[...], preferred_element_type=jnp.float32)
+    all_dz = jnp.concatenate([dz[j] for j in range(dz.shape[0])], axis=1)
+    grad[...] = jnp.dot(all_dz, x[...], preferred_element_type=jnp.float32)
     for lo, size in row_chunks(grad.shape[0], ADAM_ROWS):
         part = slice(lo, lo + size)
         new_e, m_o[part, :], v_o[part, :] = adam_step(e[part, :].astype(jnp.float32), grad[part, :], m[part, :], v[part, :], WEIGHT_DECAY)
@@ -549,7 +551,7 @@
         update_kernel,
         name="update",
         grid=(pl.cdiv(vocab, vt),),
-        in_specs=[pl.BlockSpec((vt, toks), lambda i: (i, 0)), pl.BlockSpec((toks, dim), lambda i: (0, 0)), tile, tile, tile],
+        in_specs=[pl.BlockSpec((dz.shape[0], vt, dz.shape[2]), lambda i: (0, i, 0)), pl.BlockSpec((toks, dim), lambda i: (0, 0)), tile, tile, tile],
         out_specs=(tile, tile, tile),
         out_shape=(jax.ShapeDtypeStruct((vocab, dim), bf16), jax.ShapeDtypeStruct((vocab, dim), f32), jax.ShapeDtypeStruct((vocab, dim), f32)),
         scratch_shapes=[pltpu.VMEM((vt, dim), f32)],

time: 222 us -> 222 us (level)
  no operation moved by 1% of the time
where the time goes in v4:
time: 222 us
  Pallas kernels  216 us (97%)
  other arithmetic  2.61 us (1%)
    pallas_call x1, Pallas kernels, backward(): pl.pallas_call(functools.partial(backward_kernel, n), name='backward', ou...  80.4 us
    pallas_call x1, Pallas kernels, forward(): pl.pallas_call(functools.partial(forward_kernel, n, tiles), name='forward...  72.3 us
    pallas_call x1, Pallas kernels, update(): pl.pallas_call(update_kernel, name='update', grid=(pl.cdiv(vocab, vt),),...  63.4 us

profile of v4, /device:TPU:113, one launch (start us, length us, event | category | flops | bytes accessed | tf_op | source)
XLA Modules:
  0.0 222.1 jit_solution(9952246642004252625)
XLA Ops:
  0.6 1.3 pad_add_fusion.tm
  1.9 72.3 %forward.1 = (f32[16,6288,256]{2,1,0:T(8,128)}, bf16[8,512,768]{2,1,0:T(8,128)(2,1)}, f32[16,1,256]{2,1,0:T(1,128)}, f32[16,1,256]{2,1,0:T(1,128)}, s32[16,1,256...) custom-call(bf16[512,768]{1,0:T(8,128)(2,1)} %hid.3, s32[2,512]{1,0:T(2,128)} %pad_add_fusion.tm, f32[2,768]{1,0:T(2,128)} %lnp.3, ...), custom_call_target="tpu_custom_call" | custom-call | flops 39560675328 | bytes 103022592 | tf_op jit(solution)/shard_map/forward/pallas_call | solution.py:306
  74.3 0.0 copy-start.1
  74.3 0.0 copy-start.2
  74.3 0.0 copy-start.3
  74.3 80.4 %backward.1 = (bf16[16,6288,256]{2,1,0:T(8,128)(2,1)}, bf16[512,768]{1,0:T(8,128)(2,1)}, f32[2,768]{1,0:T(2,128)}) custom-call(bf16[512,768]{1,0:T(8,128)(2,1)} %hid.3, f32[2,768]{1,0:T(2,128)} %lnp.3, f32[16,1,256]{2,1,0:T(1,128)} %get-tuple-element.24.lse, f32[16,1,256]{2,1,0:T(1,128)} %get-tuple-element.25.scale, s32[16,1,256]{2,1,0:T(1,128)} %get-tuple-element.26.tgt, ...), custom_call_target="tpu_custom_call" | custom-call | flops 39560675328 | bytes 154533888 | tf_op jit(solution)/shard_map/backward/pallas_call | solution.py:507
  154.8 0.0 copy-done.1
  154.8 0.0 copy-done.2
  154.8 0.0 copy-done.3
  154.8 1.3 divide_subtract_fusion
  156.1 0.0 copy-start.4
  156.1 0.0 copy-start.5
  156.1 0.0 copy-start
  156.1 63.4 %update.1 = (bf16[6288,768]{1,0:T(8,128)(2,1)}, f32[6288,768]{1,0:T(8,128)}, f32[6288,768]{1,0:T(8,128)}) custom-call(bf16[16,6288,256]{2,1,0:T(8,128)(2,1)} %get-tuple-element.30.dz, bf16[4096,768]{1,0:T(8,128)(2,1)} %bitcast.9, bf16[6288,768]{1,0:T(8,128)(2,1)} %e.1, f32[6288,768]{1,0:T(8,128)} %m.1, f32[6288,768]{1,0:T(8,128)} %v.1), custom_call_target="tpu_custom_call" | custom-call | flops 39560675328 | bytes 148094976 | tf_op jit(solution)/shard_map/update/pallas_call | solution.py:550
  219.5 0.0 copy-done.4
  219.5 0.6 copy.21
  220.1 0.0 copy-done.5
  220.1 0.0 copy-done
  220.1 0.9 copy.23
Async XLA Ops:
  74.3 80.5 %copy-start.1 = (f32[2,768]{1,0:T(2,128)S(1)}, f32[2,768]{1,0:T(2,128)}, u32[]{:S(2)}) copy-start(f32[2,768]{1,0:T(2,128)} %lnp.3) | copy-start | bytes 18436
  74.3 80.5 %copy-start.2 = (f32[2,768]{1,0:T(2,128)S(1)}, f32[2,768]{1,0:T(2,128)}, u32[]{:S(2)}) copy-start(f32[2,768]{1,0:T(2,128)} %param.14) | copy-start | bytes 18436
  74.3 80.5 %copy-start.3 = (f32[2,768]{1,0:T(2,128)S(1)}, f32[2,768]{1,0:T(2,128)}, u32[]{:S(2)}) copy-start(f32[2,768]{1,0:T(2,128)} %param.15) | copy-start | bytes 18436
  156.1 63.4 %copy-start.4 = (f32[1,512]{1,0:T(1,128)S(1)}, f32[1,512]{1,0:T(1,128)}, u32[]{:S(2)}) copy-start(f32[1,512]{1,0:T(1,128)} %get-tuple-element.22) | copy-start | bytes 6148
  156.1 64.0 %copy-start.5 = (f32[1,128]{1,0:T(1,128)S(1)}, f32[1,128]{1,0:T(1,128)}, u32[]{:S(2)}) copy-start(f32[1,128]{1,0:T(1,128)} %get-tuple-element.23) | copy-start | bytes 1540
  156.1 64.0 %copy-start = (bf16[512,768]{1,0:T(8,128)(2,1)S(1)}, bf16[512,768]{1,0:T(8,128)(2,1)}, u32[]{:S(2)}) copy-start(bf16[512,768]{1,0:T(8,128)(2,1)} %get-tuple-element.49) | copy-start | bytes 2359300

commit v5 on v4

--- a/solution.py
+++ b/solution.py
@@ -18,7 +18,7 @@
 MESH = pl.DeviceIdType.MESH
 VMEM_LIMIT = 64_000_000
 NEG = -3.0e38
-STAT_ROWS = 64
+STAT_ROWS = 32
 ADAM_ROWS = 16
 DZ_ROWS = 64
 DOT_ROWS = 1056
@@ -102,8 +102,6 @@
     for c in tm_copies:
         c.start()
     s1.start()
-    for c in tm_copies:
-        c.wait()
 
     def block_of(p):
         q = lax.rem(p, 2)
@@ -180,6 +178,8 @@
         def _():
             @pl.when(p == 1)
             def _():
+                for c in tm_copies:
+                    c.wait()
                 s0.wait_recv()
 
             @pl.when(p == 2)

time: 222 us -> 217 us (0.977)
  Pallas kernels: 216 us -> 211 us
    pallas_call x1, Pallas kernels: 72.3 us -> 67.2 us  [forward(): pl.pallas_call(functools.partial(forward_kernel, n, tiles), name='forward...]
where the time goes in v5:
time: 217 us
  Pallas kernels  211 us (97%)
  other arithmetic  2.61 us (1%)
    pallas_call x1, Pallas kernels, backward(): pl.pallas_call(functools.partial(backward_kernel, n), name='backward', ou...  80.5 us
    pallas_call x1, Pallas kernels, forward(): pl.pallas_call(functools.partial(forward_kernel, n, tiles), name='forward...  67.2 us
    pallas_call x1, Pallas kernels, update(): pl.pallas_call(update_kernel, name='update', grid=(pl.cdiv(vocab, vt),),...  63.4 us

profile of v5, /device:TPU:113, one launch (start us, length us, event | category | flops | bytes accessed | tf_op | source)
XLA Modules:
  0.0 217.1 jit_solution(15165577698345149403)
XLA Ops:
  0.6 1.3 pad_add_fusion.tm
  1.9 67.2 %forward.1 = (f32[16,6288,256]{2,1,0:T(8,128)}, bf16[8,512,768]{2,1,0:T(8,128)(2,1)}, f32[16,1,256]{2,1,0:T(1,128)}, f32[16,1,256]{2,1,0:T(1,128)}, s32[16,1,256...) custom-call(bf16[512,768]{1,0:T(8,128)(2,1)} %hid.3, s32[2,512]{1,0:T(2,128)} %pad_add_fusion.tm, f32[2,768]{1,0:T(2,128)} %lnp.3, ...), custom_call_target="tpu_custom_call" | custom-call | flops 39560675328 | bytes 103022592 | tf_op jit(solution)/shard_map/forward/pallas_call | solution.py:306
  69.1 0.0 copy-start.1
  69.1 0.0 copy-start.2
  69.1 0.0 copy-start.3
  69.2 80.5 %backward.1 = (bf16[16,6288,256]{2,1,0:T(8,128)(2,1)}, bf16[512,768]{1,0:T(8,128)(2,1)}, f32[2,768]{1,0:T(2,128)}) custom-call(bf16[512,768]{1,0:T(8,128)(2,1)} %hid.3, f32[2,768]{1,0:T(2,128)} %lnp.3, f32[16,1,256]{2,1,0:T(1,128)} %get-tuple-element.24.lse, f32[16,1,256]{2,1,0:T(1,128)} %get-tuple-element.25.scale, s32[16,1,256]{2,1,0:T(1,128)} %get-tuple-element.26.tgt, ...), custom_call_target="tpu_custom_call" | custom-call | flops 39560675328 | bytes 154533888 | tf_op jit(solution)/shard_map/backward/pallas_call | solution.py:507
  149.7 0.0 copy-done.1
  149.7 0.0 copy-done.2
  149.7 0.0 copy-done.3
  149.7 1.3 divide_subtract_fusion
  151.0 0.0 copy-start.4
  151.0 0.0 copy-start.5
  151.0 0.0 copy-start
  151.0 63.4 %update.1 = (bf16[6288,768]{1,0:T(8,128)(2,1)}, f32[6288,768]{1,0:T(8,128)}, f32[6288,768]{1,0:T(8,128)}) custom-call(bf16[16,6288,256]{2,1,0:T(8,128)(2,1)} %get-tuple-element.30.dz, bf16[4096,768]{1,0:T(8,128)(2,1)} %bitcast.9, bf16[6288,768]{1,0:T(8,128)(2,1)} %e.1, f32[6288,768]{1,0:T(8,128)} %m.1, f32[6288,768]{1,0:T(8,128)} %v.1), custom_call_target="tpu_custom_call" | custom-call | flops 39560675328 | bytes 148094976 | tf_op jit(solution)/shard_map/update/pallas_call | solution.py:550
  214.4 0.0 copy-done.4
  214.4 0.6 copy.21
  215.0 0.0 copy-done.5
  215.0 0.0 copy-done
  215.0 0.9 copy.23
Async XLA Ops:
  69.1 80.5 %copy-start.1 = (f32[2,768]{1,0:T(2,128)S(1)}, f32[2,768]{1,0:T(2,128)}, u32[]{:S(2)}) copy-start(f32[2,768]{1,0:T(2,128)} %lnp.3) | copy-start | bytes 18436
  69.1 80.5 %copy-start.2 = (f32[2,768]{1,0:T(2,128)S(1)}, f32[2,768]{1,0:T(2,128)}, u32[]{:S(2)}) copy-start(f32[2,768]{1,0:T(2,128)} %param.14) | copy-start | bytes 18436
  69.1 80.5 %copy-start.3 = (f32[2,768]{1,0:T(2,128)S(1)}, f32[2,768]{1,0:T(2,128)}, u32[]{:S(2)}) copy-start(f32[2,768]{1,0:T(2,128)} %param.15) | copy-start | bytes 18436
  151.0 63.4 %copy-start.4 = (f32[1,512]{1,0:T(1,128)S(1)}, f32[1,512]{1,0:T(1,128)}, u32[]{:S(2)}) copy-start(f32[1,512]{1,0:T(1,128)} %get-tuple-element.22) | copy-start | bytes 6148
  151.0 64.0 %copy-start.5 = (f32[1,128]{1,0:T(1,128)S(1)}, f32[1,128]{1,0:T(1,128)}, u32[]{:S(2)}) copy-start(f32[1,128]{1,0:T(1,128)} %get-tuple-element.23) | copy-start | bytes 1540
  151.0 64.0 %copy-start = (bf16[512,768]{1,0:T(8,128)(2,1)S(1)}, bf16[512,768]{1,0:T(8,128)(2,1)}, u32[]{:S(2)}) copy-start(bf16[512,768]{1,0:T(8,128)(2,1)} %get-tuple-element.49) | copy-start | bytes 2359300

commit v6 on v5

--- a/solution.py
+++ b/solution.py
@@ -544,7 +544,7 @@
 def update(dz, x, out_embed, mom1, mom2):
     vocab, dim = out_embed.shape
     toks = x.shape[0]
-    vt = 640
+    vt = 800
     f32, bf16 = jnp.float32, jnp.bfloat16
     tile = pl.BlockSpec((vt, dim), lambda i: (i, 0))
     return pl.pallas_call(

time: 217 us -> 217 us (level)
  no operation moved by 1% of the time
where the time goes in v6:
time: 217 us
  Pallas kernels  211 us (97%)
  other arithmetic  2.61 us (1%)
    pallas_call x1, Pallas kernels, backward(): pl.pallas_call(functools.partial(backward_kernel, n), name='backward', ou...  80.5 us
    pallas_call x1, Pallas kernels, forward(): pl.pallas_call(functools.partial(forward_kernel, n, tiles), name='forward...  67.2 us
    pallas_call x1, Pallas kernels, update(): pl.pallas_call(update_kernel, name='update', grid=(pl.cdiv(vocab, vt),),...  63 us

profile of v6, /device:TPU:113, one launch (start us, length us, event | category | flops | bytes accessed | tf_op | source)
XLA Modules:
  0.0 216.7 jit_solution(8601106021255570509)
XLA Ops:
  0.6 1.3 pad_add_fusion.tm
  1.9 67.2 %forward.1 = (f32[16,6288,256]{2,1,0:T(8,128)}, bf16[8,512,768]{2,1,0:T(8,128)(2,1)}, f32[16,1,256]{2,1,0:T(1,128)}, f32[16,1,256]{2,1,0:T(1,128)}, s32[16,1,256...) custom-call(bf16[512,768]{1,0:T(8,128)(2,1)} %hid.3, s32[2,512]{1,0:T(2,128)} %pad_add_fusion.tm, f32[2,768]{1,0:T(2,128)} %lnp.3, ...), custom_call_target="tpu_custom_call" | custom-call | flops 39560675328 | bytes 103022592 | tf_op jit(solution)/shard_map/forward/pallas_call | solution.py:306
  69.1 0.0 copy-start.1
  69.1 0.0 copy-start.2
  69.1 0.0 copy-start.3
  69.2 80.5 %backward.1 = (bf16[16,6288,256]{2,1,0:T(8,128)(2,1)}, bf16[512,768]{1,0:T(8,128)(2,1)}, f32[2,768]{1,0:T(2,128)}) custom-call(bf16[512,768]{1,0:T(8,128)(2,1)} %hid.3, f32[2,768]{1,0:T(2,128)} %lnp.3, f32[16,1,256]{2,1,0:T(1,128)} %get-tuple-element.24.lse, f32[16,1,256]{2,1,0:T(1,128)} %get-tuple-element.25.scale, s32[16,1,256]{2,1,0:T(1,128)} %get-tuple-element.26.tgt, ...), custom_call_target="tpu_custom_call" | custom-call | flops 39560675328 | bytes 154533888 | tf_op jit(solution)/shard_map/backward/pallas_call | solution.py:507
  149.7 0.0 copy-done.1
  149.7 0.0 copy-done.2
  149.7 0.0 copy-done.3
  149.7 1.3 divide_subtract_fusion
  151.0 0.0 copy-start.4
  151.0 0.0 copy-start.5
  151.0 0.0 copy-start
  151.0 63.0 %update.1 = (bf16[6288,768]{1,0:T(8,128)(2,1)}, f32[6288,768]{1,0:T(8,128)}, f32[6288,768]{1,0:T(8,128)}) custom-call(bf16[16,6288,256]{2,1,0:T(8,128)(2,1)} %get-tuple-element.30.dz, bf16[4096,768]{1,0:T(8,128)(2,1)} %bitcast.9, bf16[6288,768]{1,0:T(8,128)(2,1)} %e.1, f32[6288,768]{1,0:T(8,128)} %m.1, f32[6288,768]{1,0:T(8,128)} %v.1), custom_call_target="tpu_custom_call" | custom-call | flops 39560675328 | bytes 148094976 | tf_op jit(solution)/shard_map/update/pallas_call | solution.py:550
  214.0 0.0 copy-done.4
  214.0 0.6 copy.21
  214.6 0.0 copy-done.5
  214.7 0.0 copy-done
  214.7 0.9 copy.23
Async XLA Ops:
  69.1 80.5 %copy-start.1 = (f32[2,768]{1,0:T(2,128)S(1)}, f32[2,768]{1,0:T(2,128)}, u32[]{:S(2)}) copy-start(f32[2,768]{1,0:T(2,128)} %lnp.3) | copy-start | bytes 18436
  69.1 80.5 %copy-start.2 = (f32[2,768]{1,0:T(2,128)S(1)}, f32[2,768]{1,0:T(2,128)}, u32[]{:S(2)}) copy-start(f32[2,768]{1,0:T(2,128)} %param.14) | copy-start | bytes 18436
  69.1 80.5 %copy-start.3 = (f32[2,768]{1,0:T(2,128)S(1)}, f32[2,768]{1,0:T(2,128)}, u32[]{:S(2)}) copy-start(f32[2,768]{1,0:T(2,128)} %param.15) | copy-start | bytes 18436
  151.0 63.0 %copy-start.4 = (f32[1,512]{1,0:T(1,128)S(1)}, f32[1,512]{1,0:T(1,128)}, u32[]{:S(2)}) copy-start(f32[1,512]{1,0:T(1,128)} %get-tuple-element.22) | copy-start | bytes 6148
  151.0 63.6 %copy-start.5 = (f32[1,128]{1,0:T(1,128)S(1)}, f32[1,128]{1,0:T(1,128)}, u32[]{:S(2)}) copy-start(f32[1,128]{1,0:T(1,128)} %get-tuple-element.23) | copy-start | bytes 1540
  151.0 63.7 %copy-start = (bf16[512,768]{1,0:T(8,128)(2,1)S(1)}, bf16[512,768]{1,0:T(8,128)(2,1)}, u32[]{:S(2)}) copy-start(bf16[512,768]{1,0:T(8,128)(2,1)} %get-tuple-element.49) | copy-start | bytes 2359300
